TPU v7x, 32 devices: a whole 2x2x4 slice. The times are simulated.
32 devices in a mesh: section: 4 (over z), tensor: 8 (over y, x, core).
Axes of the slice: x: 2, y: 2, z: 4, core: 2. Of those that a mesh axis runs over, the one named last changes fastest.
Arguments:
- hidden_state: bfloat16 [64, 8192], P('section'), may hold values from -6 to 6
- norm_gain: float32 [8192], replicated, may hold values from 0.5 to 1.5
- wq_old: bfloat16 [8192, 8192], P('section', 'tensor'), may hold values from -0.0625 to 0.0625
- wkv_old: bfloat16 [8192, 2048], P('tensor', 'section'), may hold values from -0.0625 to 0.0625
- kv_old: bfloat16 [8, 4096, 16, 256], P('section', 'tensor'), may hold values from -241 to 241
- page_table: int32 [64, 64], replicated, may hold values from 0 to 4095, as said below
- lengths: int32 [64], replicated, may hold values from 1 to 1023
Outputs:
- context: bfloat16 [64, 8192], P('section', 'tensor')
- kv_new: bfloat16 [64, 8, 1024, 256], P('section', 'tensor')
- wq_new: bfloat16 [8192, 8192], P(None, 'tensor')
- wkv_new: bfloat16 [8192, 2048], P(None, 'tensor')
Inputs may be any that keep to these rules, and one draw needn't show every extreme that they name: `page_table`: every pool page belongs to exactly one page of one request. Each block of 512 consecutive pool pages holds exactly 8 pages of every request.
All inputs are finite; a program needn't handle non-finite values.
Results may differ from a plain program's by a relative error of at most 0.0075.
The roundings to bfloat16 on the way count: a program that leaves them out, or rounds other values in their place, can miss the bound.
Values may be sent and summed in bfloat16 or wider, within the bound.
A program may use at most 128 MiB of HBM per device.

v0:
```python
import functools

import jax
import jax.numpy as jnp
from jax import lax
from jax.experimental import pallas as pl
from jax.experimental.pallas import tpu as pltpu
from jax.sharding import PartitionSpec as P

KV_HEADS = 8
HEAD_DIM = 128


EPSILON = 1e-05
ROPE_BASE = 500000.0
MESH = pl.DeviceIdType.MESH
CHUNKS = 8


def rotate(values, position, head_dim):
    half = head_dim // 2
    frequency = ROPE_BASE ** (-(jnp.arange(half, dtype=jnp.float32) * 2.0 / head_dim))
    angles = position.astype(jnp.float32)[:, None] * frequency[None, :]
    cosine = jnp.cos(angles)[:, None, :]
    sine = jnp.sin(angles)[:, None, :]
    first = values[..., :half]
    second = values[..., half:]
    return jnp.concatenate(
        [first * cosine - second * sine, second * cosine + first * sine], axis=-1
    )


def pick_kernel(count, spots_ref, kv_ref, out_ref):
    base = pl.program_id(1) * count

    def step(i, carry):
        out_ref[0, 0, i] = kv_ref[0, spots_ref[base + i]]
        return carry

    lax.fori_loop(0, count, step, 0, unroll=8)


def pick_pages(kv_old, spots, sections):
    heads, pool, page, width = kv_old.shape
    count = spots.shape[0] // sections
    return pl.pallas_call(
        functools.partial(pick_kernel, count),
        out_shape=jax.ShapeDtypeStruct((sections, heads, count, page, width), kv_old.dtype),
        grid_spec=pltpu.PrefetchScalarGridSpec(
            num_scalar_prefetch=1,
            grid=(heads, sections),
            in_specs=[pl.BlockSpec((1, pool, page, width), lambda h, s, spots: (h, 0, 0, 0))],
            out_specs=pl.BlockSpec(
                (1, 1, count, page, width), lambda h, s, spots: (s, h, 0, 0, 0)
            ),
        ),
        compiler_params=pltpu.CompilerParams(vmem_limit_bytes=40 * 2**20),
        name="pick_pages",
    )(spots, kv_old)


def exchange_kernel(
    sections,
    tensors,
    local_heads,
    repeats,
    normed_ref,
    wq_ref,
    pages_ref,
    wkv_ref,
    query_ref,
    arrived_ref,
    wkv_new_ref,
    wq_new_ref,
    stage_ref,
    stage_wkv_ref,
    spread,
    part,
    partial_in,
    spread_send,
    spread_recv,
    part_send,
    part_recv,
    page_send,
    page_recv,
    wkv_send,
    wkv_recv,
    local_sem,
    own_send,
    relay_send,
    wq_recv,
    stage_send,
    stage_recv,
):
    me = lax.axis_index("section")
    mine = lax.axis_index("tensor")
    depth, columns = wq_ref.shape
    width = wkv_new_ref.shape[1]
    block = wkv_ref.shape[0]

    def spread_copy(other, slot):
        return pltpu.make_async_remote_copy(
            normed_ref.at[:, pl.ds(pl.multiple_of(other * depth, 128), depth)],
            spread.at[me],
            spread_send.at[slot],
            spread_recv.at[me],
            device_id=(other, mine),
            device_id_type=MESH,
        )

    def part_copy(other, slot):
        return pltpu.make_async_remote_copy(
            part.at[other],
            partial_in.at[me],
            part_send.at[slot],
            part_recv.at[me],
            device_id=(other, mine),
            device_id_type=MESH,
        )

    chunks = own_send.shape[1]
    chunk = depth // chunks

    def wq_rows(owner, i):
        return wq_new_ref.at[pl.ds(pl.multiple_of(owner * depth + i * chunk, 16), chunk), :]

    def own_copy(side, i):
        return pltpu.make_async_remote_copy(
            wq_ref.at[pl.ds(pl.multiple_of(i * chunk, 16), chunk), :],
            wq_rows(me, i),
            own_send.at[side, i],
            wq_recv.at[me, i],
            device_id=(me + (1, -1)[side], mine),
            device_id_type=MESH,
        )

    def relay_copy(owner, side, i):
        return pltpu.make_async_remote_copy(
            wq_rows(owner, i),
            wq_rows(owner, i),
            relay_send.at[owner, i],
            wq_recv.at[owner, i],
            device_id=(me + (1, -1)[side], mine),
            device_id_type=MESH,
        )

    onward = (me + 1 < sections, me > 0)

    def each_chunk(act):
        def run(i, carry):
            act(i)
            return carry

        lax.fori_loop(0, chunks, run, 0)

    for step in range(1, sections):
        spread_copy(lax.rem(me + step, sections), step).start()

    def send_own(i):
        for side in range(2):
            pl.when(onward[side])(lambda: own_copy(side, i).start())

    def stage_copy(origin, other, step, which):
        pairs = (
            (pages_ref.at[other], stage_ref.at[origin]),
            (wkv_ref, stage_wkv_ref.at[origin]),
        )
        return pltpu.make_async_remote_copy(
            *pairs[which],
            stage_send.at[which, step],
            stage_recv.at[which, origin],
            device_id=(other, mine),
            device_id_type=MESH,
        )

    for step in range(1, sections):
        for which in range(2):
            stage_copy(me, lax.rem(me + step, sections), step, which).start()
    each_chunk(send_own)
    keep = pltpu.make_async_copy(
        wq_ref, wq_new_ref.at[pl.ds(pl.multiple_of(me * depth, 16), depth), :], local_sem.at[2]
    )
    keep.start()
    spread[me] = normed_ref[:, pl.ds(pl.multiple_of(me * depth, 128), depth)]

    def page_copy(step, head, copy):
        slot = (step * local_heads + head) * repeats + copy
        other = lax.rem(me + step, sections)
        target = (other * local_heads + head) * repeats + copy
        source = pages_ref.at[me, head] if step == 0 else stage_ref.at[other, head]
        here = (source, arrived_ref.at[mine])
        remote = pltpu.make_async_remote_copy(
            *here,
            page_send.at[slot],
            page_recv.at[mine],
            device_id=(me, target),
            device_id_type=MESH,
        )
        return target, remote, pltpu.make_async_copy(*here, local_sem.at[0])

    def wkv_copy(step, head, copy):
        slot = (step * local_heads + head) * repeats + copy
        other = lax.rem(me + step, sections)
        target = (other * local_heads + head) * repeats + copy
        here = (
            (wkv_ref if step == 0 else stage_wkv_ref.at[other]).at[:, pl.ds(head * width, width)],
            wkv_new_ref.at[pl.ds(pl.multiple_of(mine * block, 128), block), :],
        )
        remote = pltpu.make_async_remote_copy(
            *here,
            wkv_send.at[slot],
            wkv_recv.at[mine],
            device_id=(me, target),
            device_id_type=MESH,
        )
        return target, remote, pltpu.make_async_copy(*here, local_sem.at[1])

    every = [
        (make, step % sections, head, copy)
        for make in (page_copy, wkv_copy)
        for step in range(1, sections + 1)
        for head in range(local_heads)
        for copy in range(repeats)
    ]
    def begin(chosen):
        for make, step, head, copy in every:
            if step == chosen:
                target, remote, local = make(step, head, copy)
                pl.when(target != mine)(remote.start)
                pl.when(target == mine)(local.start)

    begin(0)

    for step in range(1, sections):
        other = lax.rem(me + step, sections)
        spread_copy(other, step).wait_send()
        pltpu.make_async_remote_copy(
            spread.at[other],
            spread.at[other],
            spread_send.at[step],
            spread_recv.at[other],
            device_id=(other, mine),
            device_id_type=MESH,
        ).wait_recv()

    tile = 256

    def product(i, carry):
        group = i // (columns // tile)
        span = pl.ds(pl.multiple_of(lax.rem(i, columns // tile) * tile, tile), tile)
        part[group, :, span] = jnp.dot(
            spread[group], wq_ref[:, span], preferred_element_type=jnp.float32
        )
        return carry

    lax.fori_loop(0, sections * (columns // tile), product, 0)
    for step in range(1, sections):
        part_copy(lax.rem(me + step, sections), step).start()
    partial_in[me] = part[me]

    for step in range(1, sections):
        other = lax.rem(me + step, sections)
        for which in range(2):
            stage_copy(me, other, step, which).wait_send()
            stage_copy(other, other, step, which).wait_recv()
        begin(step)

    for step in range(1, sections):

        def pass_on(i):
            for side in range(2):
                owner = me - step if side == 0 else me + step
                real = owner >= 0 if side == 0 else owner < sections

                @pl.when(real)
                def _():
                    relay_copy(owner, side, i).wait_recv()
                    pl.when(onward[side])(lambda: relay_copy(owner, side, i).start())

        each_chunk(pass_on)

    for step in range(1, sections):
        other = lax.rem(me + step, sections)
        part_copy(other, step).wait_send()
        pltpu.make_async_remote_copy(
            part.at[other],
            partial_in.at[other],
            part_send.at[step],
            part_recv.at[other],
            device_id=(other, mine),
            device_id_type=MESH,
        ).wait_recv()
    total = partial_in[0]
    for group in range(1, sections):
        total = total + partial_in[group]
    query_ref[...] = total

    keep.wait()

    def sent(i):
        for side in range(2):
            pl.when(onward[side])(lambda: own_copy(side, i).wait_send())
            for step in range(1, sections):
                owner = me - step if side == 0 else me + step
                real = owner >= 0 if side == 0 else owner < sections
                pl.when(jnp.logical_and(real, onward[side]))(
                    lambda: relay_copy(owner, side, i).wait_send()
                )

    each_chunk(sent)
    for make, step, head, copy in every:
        target, remote, local = make(step, head, copy)
        pl.when(target != mine)(remote.wait_send)
        pl.when(target == mine)(local.wait)
    for origin in range(tensors):
        pages_in = pltpu.make_async_remote_copy(
            pages_ref.at[0, 0],
            arrived_ref.at[origin],
            page_send.at[0],
            page_recv.at[origin],
            device_id=(me, origin),
            device_id_type=MESH,
        )
        wkv_in = pltpu.make_async_remote_copy(
            wkv_ref.at[:, pl.ds(0, width)],
            wkv_new_ref.at[pl.ds(origin * block, block), :],
            wkv_send.at[0],
            wkv_recv.at[origin],
            device_id=(me, origin),
            device_id_type=MESH,
        )
        outside = mine != origin
        pl.when(outside)(pages_in.wait_recv)
        pl.when(outside)(wkv_in.wait_recv)


def exchange(normed, wq_old, pages, wkv_old, sections, tensors, repeats):
    rows = normed.shape[0]
    depth, columns = wq_old.shape
    local_heads = pages.shape[1]
    width = pages.shape[4]
    copies = sections * local_heads * repeats
    dma = pltpu.SemaphoreType.DMA
    vmem = pl.BlockSpec(memory_space=pltpu.VMEM)
    hbm = pl.BlockSpec(memory_space=pl.ANY)
    return pl.pallas_call(
        functools.partial(exchange_kernel, sections, tensors, local_heads, repeats),
        out_shape=(
            jax.ShapeDtypeStruct((rows, columns), jnp.float32),
            jax.ShapeDtypeStruct((tensors,) + pages.shape[2:], pages.dtype),
            jax.ShapeDtypeStruct((wkv_old.shape[0] * tensors, width), wkv_old.dtype),
            jax.ShapeDtypeStruct((depth * sections, columns), wq_old.dtype),
            jax.ShapeDtypeStruct(pages.shape, pages.dtype),
            jax.ShapeDtypeStruct((sections,) + wkv_old.shape, wkv_old.dtype),
        ),
        in_specs=[vmem, vmem, hbm, hbm],
        out_specs=(vmem, hbm, hbm, hbm, hbm, hbm),
        scratch_shapes=[
            pltpu.VMEM((sections, rows, depth), normed.dtype),
            pltpu.VMEM((sections, rows, columns), jnp.float32),
            pltpu.VMEM((sections, rows, columns), jnp.float32),
            dma((sections,)),
            dma((sections,)),
            dma((sections,)),
            dma((sections,)),
            dma((copies,)),
            dma((tensors,)),
            dma((copies,)),
            dma((tensors,)),
            dma((3,)),
            dma((2, CHUNKS)),
            dma((sections, CHUNKS)),
            dma((sections, CHUNKS)),
            dma((2, sections)),
            dma((2, sections)),
        ],
        compiler_params=pltpu.CompilerParams(
            has_side_effects=True, vmem_limit_bytes=40 * 2**20
        ),
        cost_estimate=pl.CostEstimate(
            flops=2 * sections * rows * depth * columns,
            bytes_accessed=400 * 2**20,
            transcendentals=0,
        ),
        name="exchange",
    )(normed, wq_old, pages, wkv_old)


def attend_kernel(
    pages_of, per_block, page, head_dim, place_ref, length_ref, in_ref, fresh_ref, query_ref, cache_ref, context_ref
):
    request = pl.program_id(0)
    length = length_ref[request]
    base = request * pages_of

    def order(j, carry):
        spot = place_ref[base + j]
        start = pl.multiple_of(j * page, page)
        cache_ref[0, pl.ds(start, page), :] = in_ref[
            lax.div(spot, per_block), 0, lax.rem(spot, per_block)
        ]
        return carry

    lax.fori_loop(0, pages_of, order, 0, unroll=8)
    start = pl.multiple_of(lax.div(length, page) * page, page)
    held = cache_ref[0, pl.ds(start, page), :]
    row = lax.broadcasted_iota(jnp.int32, held.shape, 0)
    fresh = jnp.broadcast_to(fresh_ref[0].astype(jnp.float32), held.shape)
    cache_ref[0, pl.ds(start, page), :] = jnp.where(
        row == lax.rem(length, page), fresh, held.astype(jnp.float32)
    ).astype(held.dtype)
    keys = cache_ref[0, :, :head_dim]
    values = cache_ref[0, :, head_dim:]
    scores = lax.dot_general(
        query_ref[0], keys, (((1,), (1,)), ((), ())), preferred_element_type=jnp.float32
    ) * head_dim ** (-0.5)
    seen = lax.broadcasted_iota(jnp.int32, scores.shape, 1) <= length
    peak = jnp.max(jnp.where(seen, scores, -jnp.inf), axis=1, keepdims=True)
    weights = jnp.where(seen, jnp.exp(scores - peak), 0.0)
    probs = (weights / jnp.sum(weights, axis=1, keepdims=True)).astype(jnp.bfloat16)
    context_ref[0] = jnp.dot(probs, values, preferred_element_type=jnp.float32).astype(
        context_ref.dtype
    )


def attend(arrived, place, lengths, fresh, query, head_dim):
    blocks, rows, per_block, page, width = arrived.shape
    pages_of = blocks * per_block
    heads = query.shape[1]
    return pl.pallas_call(
        functools.partial(attend_kernel, pages_of, per_block, page, head_dim),
        out_shape=(
            jax.ShapeDtypeStruct((rows, pages_of * page, width), arrived.dtype),
            jax.ShapeDtypeStruct(query.shape, jnp.bfloat16),
        ),
        grid_spec=pltpu.PrefetchScalarGridSpec(
            num_scalar_prefetch=2,
            grid=(rows,),
            in_specs=[
                pl.BlockSpec((blocks, 1, per_block, page, width), lambda r, *_: (0, r, 0, 0, 0)),
                pl.BlockSpec((1, 1, width), lambda r, *_: (r, 0, 0)),
                pl.BlockSpec((1, heads, head_dim), lambda r, *_: (r, 0, 0)),
            ],
            out_specs=(
                pl.BlockSpec((1, pages_of * page, width), lambda r, *_: (r, 0, 0)),
                pl.BlockSpec((1, heads, head_dim), lambda r, *_: (r, 0, 0)),
            ),
        ),
        cost_estimate=pl.CostEstimate(
            flops=4 * rows * heads * pages_of * page * head_dim,
            bytes_accessed=4 * arrived.size,
            transcendentals=rows * heads * pages_of * page,
        ),
        compiler_params=pltpu.CompilerParams(vmem_limit_bytes=40 * 2**20),
        name="attend",
    )(place.reshape(-1), lengths, arrived, fresh[:, None, :], query)


def shards(hidden_state, norm_gain, wq_old, wkv_old, kv_old, page_table, lengths):
    sections = lax.axis_size("section")
    tensors = lax.axis_size("tensor")
    section_id = lax.axis_index("section")
    tensor_id = lax.axis_index("tensor")
    rows = hidden_state.shape[0]
    head_dim = HEAD_DIM
    width = 2 * head_dim
    repeats = tensors // KV_HEADS
    queries_here = wq_old.shape[1] // head_dim
    pool_dev = kv_old.shape[1]
    page = kv_old.shape[2]
    per_block = page_table.shape[1] // tensors
    widened = hidden_state.astype(jnp.float32)
    scale = lax.rsqrt(jnp.mean(widened * widened, axis=1, keepdims=True) + EPSILON)
    normed = (widened * scale * norm_gain[None, :]).astype(jnp.bfloat16)
    owner = page_table // pool_dev
    blocks = jnp.arange(tensors, dtype=jnp.int32)
    onehot = (owner[:, :, None] == blocks[None, None, :]).astype(jnp.int32)
    ranks = jnp.sum((jnp.cumsum(onehot, axis=1) - 1) * onehot, axis=2)
    mine = owner == tensor_id
    wanted = ranks[:, :, None] == jnp.arange(per_block, dtype=jnp.int32)[None, None, :]
    picks = (mine[:, :, None] & wanted).astype(jnp.int32)
    spots = jnp.sum(picks * (page_table % pool_dev)[:, :, None], axis=1)
    pages = pick_pages(kv_old, spots.reshape(-1), sections)
    query, arrived, wkv_new, wq_new, _, _ = exchange(
        normed, wq_old, pages, wkv_old, sections, tensors, repeats
    )
    arrived = arrived.reshape(tensors, rows, per_block, page, width)
    place = lax.dynamic_slice_in_dim(owner * per_block + ranks, section_id * rows, rows, 0)
    my_lengths = lax.dynamic_slice_in_dim(lengths, section_id * rows, rows, 0)
    fresh = jnp.dot(normed, wkv_new, preferred_element_type=jnp.float32)
    fresh_key = rotate(fresh[:, None, :head_dim], my_lengths, head_dim)[:, 0]
    fresh = jnp.concatenate([fresh_key, fresh[:, head_dim:]], axis=1).astype(jnp.bfloat16)
    query = rotate(query.reshape(rows, queries_here, head_dim), my_lengths, head_dim).astype(
        jnp.bfloat16
    )
    cache, context = attend(arrived, place, my_lengths, fresh, query, head_dim)
    return (context.reshape(rows, queries_here * head_dim), cache[:, None], wq_new, wkv_new)


def solution(mesh):
    placed = (
        P("section", None),
        P(),
        P("section", "tensor"),
        P("tensor", "section"),
        P("section", "tensor", None, None),
        P(),
        P(),
    )
    return jax.shard_map(
        shards,
        mesh=mesh,
        in_specs=placed,
        out_specs=(
            P("section", "tensor"),
            P("section", "tensor", None, None),
            P(None, "tensor"),
            P(None, "tensor"),
        ),
        check_vma=False,
    )
```

profile of v0, /device:TPU:0, one launch (start us, length us, event | category | flops | bytes accessed | tf_op | source)
XLA Modules:
  0.0 549.1 jit_solution(5833586532725514584)
XLA Ops:
  0.6 0.8 copy.35
  1.5 2.3 select_reduce_fusion.1
  3.8 0.1 dynamic-slice_add_fusion
  3.9 0.1 copy.39
  3.9 0.1 reshape.170.place_ref
  4.0 0.7 fusion.10
  4.7 1.1 fusion.4
  5.9 1.1 fusion.6.normed_ref
  7.0 2.2 select_reduce_fusion
  9.2 0.1 reshape.171.spots_ref
  9.3 0.0 copy-start.2
  9.3 0.0 copy-start.3
  9.3 7.0 %pick_pages.1.pages_ref = bf16[4,2,128,16,256]{4,3,2,1,0:T(8,128)(2,1)S(1)} custom-call(s32[512]{0:T(512)S(1)} %reshape.171.spots_ref, bf16[2,512,16,256]{3,2,1,0:T(8,128)(2,1)} %kv_ref.1), custom_call_target="tpu_custom_call" | custom-call | tf_op jit(solution)/shard_map/pick_pages/pallas_call | solution.py:46
  16.3 0.0 copy-start
  16.3 3.4 copy-done
  19.7 0.0 copy-done.2
  19.7 0.0 copy-done.3
  19.7 492.0 %exchange.1 = (f32[16,1024]{1,0:T(8,128)S(1)}, bf16[8,128,16,256]{3,2,1,0:T(8,128)(2,1)}, bf16[8192,256]{1,0:T(8,128)(2,1)S(1)}, bf16[8192,1024]{1,0:T(8,128)(2,...) custom-call(bf16[16,8192]{1,0:T(8,128)(2,1)S(1)} %fusion.6.normed_ref, ...), custom_call_target="tpu_custom_call" | custom-call | flops 268435456 | bytes 419430400 | tf_op jit(solution)/shard_map/exchange/pallas_call | solution.py:346
  511.8 0.7 fusion.11
  512.5 0.1 mul.133
  512.5 0.3 subtract_convert_fusion.1
  512.8 0.1 pad_maximum_fusion.1.fresh_ref
  512.9 0.1 multiply_cosine_fusion
  513.1 0.1 subtract_convert_fusion
  513.2 0.1 pad_maximum_fusion.query_ref
  513.3 0.0 copy-start.1
  513.3 3.4 copy-done.1
  516.6 15.9 %attend.1 = (bf16[16,1024,256]{2,1,0:T(8,128)(2,1)}, bf16[16,8,128]{2,1,0:T(8,128)(2,1)S(1)}) custom-call(s32[1024]{0:T(1024)S(1)} %reshape.170.place_ref, s32[16]{0:T(128)S(1)} %get-tuple-element.37.length_ref, bf16[8,16,8,16,256]{4,3,2,1,0:T(8,128)(2,1)S(1)} %bitcast.16, bf16[16,1,256]{2,1,0:T(2,128)(2,1)S(1)} %pad_maximum_fusion.1.fresh_ref, ...), custom_call_target="tpu_custom_call" | custom-call | flops 67108864 | bytes 16777216 | tf_op jit(solution)/shard_map/attend/pallas_call | solution.py:430
  532.5 0.6 copy.46
  533.2 13.9 %copy.49 = bf16[8192,1024]{1,0:T(8,128)(2,1)} copy(bf16[8192,1024]{1,0:T(8,128)(2,1)} %get-tuple-element.52) | data formatting | bytes 33554432
  547.1 2.0 copy.50
  (8 shorter events, 0.1 us)
Async XLA Ops:
  9.3 10.4 %copy-start.2 = (bf16[2048,1024]{1,0:T(8,128)(2,1)S(1)}, bf16[2048,1024]{1,0:T(8,128)(2,1)}, u32[]{:S(2)}) copy-start(bf16[2048,1024]{1,0:T(8,128)(2,1)} %wq_ref.1) | copy-start | bytes 12582916
  9.3 10.4 %copy-start.3 = (bf16[1024,512]{1,0:T(8,128)(2,1)S(1)}, bf16[1024,512]{1,0:T(8,128)(2,1)}, u32[]{:S(2)}) copy-start(bf16[1024,512]{1,0:T(8,128)(2,1)} %wkv_ref.1) | copy-start | bytes 3145732
  16.3 3.4 copy-start
  513.3 3.4 copy-start.1
where the time goes:
time: 549 us
  Pallas kernels  515 us (94%)
  local copies, waits for them, and re-layouts  24.5 us (4%)
  other arithmetic  8.23 us (1%)
    pallas_call x1, Pallas kernels, exchange(): pl.pallas_call(functools.partial(exchange_kernel, sections, tensors, loca...  492 us
    unnamed x13, local copies, waits for them, and re-layouts  24.2 us
    pallas_call x1, Pallas kernels, attend(): pl.pallas_call(functools.partial(attend_kernel, pages_of, per_block, page...  15.9 us

commit v1 on v0

--- a/solution.py
+++ b/solution.py
@@ -7,6 +7,7 @@
 from jax.experimental.pallas import tpu as pltpu
 from jax.sharding import PartitionSpec as P
 
+
 KV_HEADS = 8
 HEAD_DIM = 128
 
@@ -15,6 +16,9 @@
 ROPE_BASE = 500000.0
 MESH = pl.DeviceIdType.MESH
 CHUNKS = 8
+TILES = 8
+EARLY = 2
+LATE = 4
 
 
 def rotate(values, position, head_dim):
@@ -64,23 +68,22 @@
     tensors,
     local_heads,
     repeats,
+    kept,
     normed_ref,
     wq_ref,
     pages_ref,
     wkv_ref,
-    query_ref,
+    part_ref,
     arrived_ref,
     wkv_new_ref,
     wq_new_ref,
     stage_ref,
     stage_wkv_ref,
+    late_ref,
+    held,
     spread,
-    part,
-    partial_in,
-    spread_send,
-    spread_recv,
-    part_send,
-    part_recv,
+    made,
+    part_in,
     page_send,
     page_recv,
     wkv_send,
@@ -91,35 +94,25 @@
     wq_recv,
     stage_send,
     stage_recv,
+    wkv_own_send,
+    wkv_relay_send,
+    wkv_stage_recv,
+    help_send,
+    help_recv,
 ):
     me = lax.axis_index("section")
     mine = lax.axis_index("tensor")
     depth, columns = wq_ref.shape
     width = wkv_new_ref.shape[1]
     block = wkv_ref.shape[0]
-
-    def spread_copy(other, slot):
-        return pltpu.make_async_remote_copy(
-            normed_ref.at[:, pl.ds(pl.multiple_of(other * depth, 128), depth)],
-            spread.at[me],
-            spread_send.at[slot],
-            spread_recv.at[me],
-            device_id=(other, mine),
-            device_id_type=MESH,
-        )
-
-    def part_copy(other, slot):
-        return pltpu.make_async_remote_copy(
-            part.at[other],
-            partial_in.at[me],
-            part_send.at[slot],
-            part_recv.at[me],
-            device_id=(other, mine),
-            device_id_type=MESH,
-        )
-
+    late_rows = late_ref.shape[0]
     chunks = own_send.shape[1]
     chunk = depth // chunks
+    last = sections - 1
+    onward = (me < last, me > 0)
+    next_to = (me + 1, me - 1)
+    feeds = (me == last - 1, me == 1)
+    fed = (me == last, me == 0)
 
     def wq_rows(owner, i):
         return wq_new_ref.at[pl.ds(pl.multiple_of(owner * depth + i * chunk, 16), chunk), :]
@@ -130,7 +123,7 @@
             wq_rows(me, i),
             own_send.at[side, i],
             wq_recv.at[me, i],
-            device_id=(me + (1, -1)[side], mine),
+            device_id=(next_to[side], mine),
             device_id_type=MESH,
         )
 
@@ -140,48 +133,61 @@
             wq_rows(owner, i),
             relay_send.at[owner, i],
             wq_recv.at[owner, i],
-            device_id=(me + (1, -1)[side], mine),
-            device_id_type=MESH,
-        )
-
-    onward = (me + 1 < sections, me > 0)
-
-    def each_chunk(act):
+            device_id=(next_to[side], mine),
+            device_id_type=MESH,
+        )
+
+    def each_chunk(act, first=0, end=chunks):
         def run(i, carry):
             act(i)
             return carry
 
-        lax.fori_loop(0, chunks, run, 0)
-
-    for step in range(1, sections):
-        spread_copy(lax.rem(me + step, sections), step).start()
+        lax.fori_loop(first, end, run, 0)
+
+    def goes(side, i):
+        return jnp.logical_and(
+            onward[side], jnp.logical_or(jnp.logical_not(feeds[side]), i < kept)
+        )
 
     def send_own(i):
         for side in range(2):
-            pl.when(onward[side])(lambda: own_copy(side, i).start())
-
-    def stage_copy(origin, other, step, which):
-        pairs = (
-            (pages_ref.at[other], stage_ref.at[origin]),
-            (wkv_ref, stage_wkv_ref.at[origin]),
-        )
+            pl.when(goes(side, i))(lambda: own_copy(side, i).start())
+
+    def owner_of(side, step):
+        return (me - step, me + step)[side]
+
+    def real(side, step):
+        return (me - step >= 0, me + step < sections)[side]
+
+    def stage_copy(origin, other, step):
         return pltpu.make_async_remote_copy(
-            *pairs[which],
-            stage_send.at[which, step],
-            stage_recv.at[which, origin],
+            pages_ref.at[other],
+            stage_ref.at[origin],
+            stage_send.at[step],
+            stage_recv.at[origin],
             device_id=(other, mine),
             device_id_type=MESH,
         )
 
-    for step in range(1, sections):
-        for which in range(2):
-            stage_copy(me, lax.rem(me + step, sections), step, which).start()
-    each_chunk(send_own)
-    keep = pltpu.make_async_copy(
-        wq_ref, wq_new_ref.at[pl.ds(pl.multiple_of(me * depth, 16), depth), :], local_sem.at[2]
-    )
-    keep.start()
-    spread[me] = normed_ref[:, pl.ds(pl.multiple_of(me * depth, 128), depth)]
+    def wkv_own_copy(side):
+        return pltpu.make_async_remote_copy(
+            wkv_ref,
+            stage_wkv_ref.at[me],
+            wkv_own_send.at[side],
+            wkv_stage_recv.at[me],
+            device_id=(next_to[side], mine),
+            device_id_type=MESH,
+        )
+
+    def wkv_relay_copy(owner, side):
+        return pltpu.make_async_remote_copy(
+            stage_wkv_ref.at[owner],
+            stage_wkv_ref.at[owner],
+            wkv_relay_send.at[owner],
+            wkv_stage_recv.at[owner],
+            device_id=(next_to[side], mine),
+            device_id_type=MESH,
+        )
 
     def page_copy(step, head, copy):
         slot = (step * local_heads + head) * repeats + copy
@@ -215,64 +221,94 @@
         )
         return target, remote, pltpu.make_async_copy(*here, local_sem.at[1])
 
-    every = [
-        (make, step % sections, head, copy)
-        for make in (page_copy, wkv_copy)
-        for step in range(1, sections + 1)
-        for head in range(local_heads)
-        for copy in range(repeats)
-    ]
-    def begin(chosen):
-        for make, step, head, copy in every:
-            if step == chosen:
+    def begin(make, step):
+        for head in range(local_heads):
+            for copy in range(repeats):
                 target, remote, local = make(step, head, copy)
                 pl.when(target != mine)(remote.start)
                 pl.when(target == mine)(local.start)
 
-    begin(0)
-
-    for step in range(1, sections):
-        other = lax.rem(me + step, sections)
-        spread_copy(other, step).wait_send()
-        pltpu.make_async_remote_copy(
-            spread.at[other],
-            spread.at[other],
-            spread_send.at[step],
-            spread_recv.at[other],
-            device_id=(other, mine),
-            device_id_type=MESH,
-        ).wait_recv()
-
+    def spread_copy(side):
+        feeder = (last - 1, 1)[side]
+        start = pl.multiple_of(feeder * depth + depth - late_rows, 128)
+        return pltpu.make_async_remote_copy(
+            normed_ref.at[:, pl.ds(start, late_rows)],
+            spread.at[side],
+            help_send.at[0],
+            help_recv.at[side],
+            device_id=(feeder, mine),
+            device_id_type=MESH,
+        )
+
+    def part_copy(side):
+        return pltpu.make_async_remote_copy(
+            made.at[side],
+            part_in,
+            help_send.at[1 + side],
+            help_recv.at[2],
+            device_id=((last, 0)[side], mine),
+            device_id_type=MESH,
+        )
+
+    for side in range(2):
+        pl.when(onward[side])(lambda: wkv_own_copy(side).start())
+        pl.when(fed[side])(lambda: spread_copy(side).start())
+    begin(wkv_copy, 0)
+    begin(page_copy, 0)
+    each_chunk(send_own)
+    for step in range(sections - 1, 0, -1):
+        for side in range(2):
+            pl.when(real(side, step))(
+                lambda: stage_copy(
+                    me, owner_of(side, step), step if side else sections - step
+                ).start()
+            )
+
+    take = pltpu.make_async_copy(
+        wq_ref.at[pl.ds(depth - late_rows, late_rows), :], held, local_sem.at[2]
+    )
+    take.start()
+    take.wait()
+    put = pltpu.make_async_copy(held, late_ref, local_sem.at[3])
+    put.start()
     tile = 256
-
-    def product(i, carry):
-        group = i // (columns // tile)
-        span = pl.ds(pl.multiple_of(lax.rem(i, columns // tile) * tile, tile), tile)
-        part[group, :, span] = jnp.dot(
-            spread[group], wq_ref[:, span], preferred_element_type=jnp.float32
-        )
-        return carry
-
-    lax.fori_loop(0, sections * (columns // tile), product, 0)
-    for step in range(1, sections):
-        part_copy(lax.rem(me + step, sections), step).start()
-    partial_in[me] = part[me]
-
-    for step in range(1, sections):
-        other = lax.rem(me + step, sections)
-        for which in range(2):
-            stage_copy(me, other, step, which).wait_send()
-            stage_copy(other, other, step, which).wait_recv()
-        begin(step)
-
-    for step in range(1, sections):
-
+    for side in range(2):
+
+        @pl.when(feeds[side])
+        def _():
+            spread_copy(side).wait_recv()
+
+            def product(i, carry):
+                span = pl.ds(pl.multiple_of(i * tile, tile), tile)
+                made[side, :, span] = jnp.dot(
+                    spread[side], held[:, span], preferred_element_type=jnp.float32
+                )
+                return carry
+
+            lax.fori_loop(0, columns // tile, product, 0)
+            part_copy(side).start()
+
+    def pass_wkv(step):
+        for side in range(2):
+            owner = owner_of(side, step)
+
+            @pl.when(real(side, step))
+            def _():
+                wkv_relay_copy(owner, side).wait_recv()
+                pl.when(onward[side])(lambda: wkv_relay_copy(owner, side).start())
+                begin(wkv_copy, step if side else sections - step)
+
+    def pass_wq(step):
         def pass_on(i):
             for side in range(2):
-                owner = me - step if side == 0 else me + step
-                real = owner >= 0 if side == 0 else owner < sections
-
-                @pl.when(real)
+                owner = owner_of(side, step)
+                there = real(side, step)
+                if step == 1:
+                    there = jnp.logical_and(
+                        there, jnp.logical_or(jnp.logical_not(fed[side]), i < kept)
+                    )
+
+                @pl.when(there)
                 def _():
                     relay_copy(owner, side, i).wait_recv()
                     pl.when(onward[side])(lambda: relay_copy(owner, side, i).start())
@@ -280,38 +316,57 @@
         each_chunk(pass_on)
 
     for step in range(1, sections):
-        other = lax.rem(me + step, sections)
-        part_copy(other, step).wait_send()
-        pltpu.make_async_remote_copy(
-            part.at[other],
-            partial_in.at[other],
-            part_send.at[step],
-            part_recv.at[other],
-            device_id=(other, mine),
-            device_id_type=MESH,
-        ).wait_recv()
-    total = partial_in[0]
-    for group in range(1, sections):
-        total = total + partial_in[group]
-    query_ref[...] = total
-
-    keep.wait()
+        pass_wkv(step)
+        pass_wq(step)
+        if step == 1:
+            for away in range(1, sections):
+                other = lax.rem(me + away, sections)
+                stage_copy(other, other, away).wait_recv()
+                begin(page_copy, away)
+
+    put.wait()
+    for side in range(2):
+
+        @pl.when(fed[side])
+        def _():
+            spread_copy(side).wait_send()
+            part_copy(side).wait_recv()
+
+        pl.when(feeds[side])(lambda: part_copy(side).wait_send())
+    end = jnp.logical_or(fed[0], fed[1])
+
+    @pl.when(end)
+    def _():
+        part_ref[...] = part_in[...]
+
+    @pl.when(jnp.logical_not(end))
+    def _():
+        part_ref[...] = jnp.zeros_like(part_ref)
 
     def sent(i):
         for side in range(2):
-            pl.when(onward[side])(lambda: own_copy(side, i).wait_send())
+            pl.when(goes(side, i))(lambda: own_copy(side, i).wait_send())
             for step in range(1, sections):
-                owner = me - step if side == 0 else me + step
-                real = owner >= 0 if side == 0 else owner < sections
-                pl.when(jnp.logical_and(real, onward[side]))(
-                    lambda: relay_copy(owner, side, i).wait_send()
+                pl.when(jnp.logical_and(real(side, step), onward[side]))(
+                    lambda: relay_copy(owner_of(side, step), side, i).wait_send()
                 )
 
     each_chunk(sent)
-    for make, step, head, copy in every:
-        target, remote, local = make(step, head, copy)
-        pl.when(target != mine)(remote.wait_send)
-        pl.when(target == mine)(local.wait)
+    for side in range(2):
+        pl.when(onward[side])(lambda: wkv_own_copy(side).wait_send())
+        for step in range(1, sections):
+            pl.when(jnp.logical_and(real(side, step), onward[side]))(
+                lambda: wkv_relay_copy(owner_of(side, step), side).wait_send()
+            )
+    for step in range(1, sections):
+        stage_copy(me, lax.rem(me + step, sections), step).wait_send()
+    for make in (page_copy, wkv_copy):
+        for step in range(sections):
+            for head in range(local_heads):
+                for copy in range(repeats):
+                    target, remote, local = make(step, head, copy)
+                    pl.when(target != mine)(remote.wait_send)
+                    pl.when(target == mine)(local.wait)
     for origin in range(tensors):
         pages_in = pltpu.make_async_remote_copy(
             pages_ref.at[0, 0],
@@ -340,11 +395,15 @@
     local_heads = pages.shape[1]
     width = pages.shape[4]
     copies = sections * local_heads * repeats
+    late_rows = depth // TILES * LATE
+    kept = CHUNKS // TILES * (TILES - EARLY - LATE)
     dma = pltpu.SemaphoreType.DMA
     vmem = pl.BlockSpec(memory_space=pltpu.VMEM)
     hbm = pl.BlockSpec(memory_space=pl.ANY)
     return pl.pallas_call(
-        functools.partial(exchange_kernel, sections, tensors, local_heads, repeats),
+        functools.partial(
+            exchange_kernel, sections, tensors, local_heads, repeats, kept
+        ),
         out_shape=(
             jax.ShapeDtypeStruct((rows, columns), jnp.float32),
             jax.ShapeDtypeStruct((tensors,) + pages.shape[2:], pages.dtype),
@@ -352,38 +411,201 @@
             jax.ShapeDtypeStruct((depth * sections, columns), wq_old.dtype),
             jax.ShapeDtypeStruct(pages.shape, pages.dtype),
             jax.ShapeDtypeStruct((sections,) + wkv_old.shape, wkv_old.dtype),
-        ),
-        in_specs=[vmem, vmem, hbm, hbm],
-        out_specs=(vmem, hbm, hbm, hbm, hbm, hbm),
+            jax.ShapeDtypeStruct((late_rows, columns), wq_old.dtype),
+        ),
+        in_specs=[vmem, hbm, hbm, hbm],
+        out_specs=(vmem, hbm, hbm, hbm, hbm, hbm, hbm),
         scratch_shapes=[
-            pltpu.VMEM((sections, rows, depth), normed.dtype),
-            pltpu.VMEM((sections, rows, columns), jnp.float32),
-            pltpu.VMEM((sections, rows, columns), jnp.float32),
-            dma((sections,)),
-            dma((sections,)),
-            dma((sections,)),
-            dma((sections,)),
+            pltpu.VMEM((late_rows, columns), wq_old.dtype),
+            pltpu.VMEM((2, rows, late_rows), normed.dtype),
+            pltpu.VMEM((2, rows, columns), jnp.float32),
+            pltpu.VMEM((rows, columns), jnp.float32),
             dma((copies,)),
             dma((tensors,)),
             dma((copies,)),
             dma((tensors,)),
-            dma((3,)),
+            dma((4,)),
             dma((2, CHUNKS)),
             dma((sections, CHUNKS)),
             dma((sections, CHUNKS)),
-            dma((2, sections)),
-            dma((2, sections)),
+            dma((sections,)),
+            dma((sections,)),
+            dma((2,)),
+            dma((sections,)),
+            dma((sections,)),
+            dma((3,)),
+            dma((3,)),
         ],
         compiler_params=pltpu.CompilerParams(
             has_side_effects=True, vmem_limit_bytes=40 * 2**20
         ),
         cost_estimate=pl.CostEstimate(
-            flops=2 * sections * rows * depth * columns,
+            flops=4 * rows * late_rows * columns,
             bytes_accessed=400 * 2**20,
             transcendentals=0,
         ),
         name="exchange",
     )(normed, wq_old, pages, wkv_old)
+
+
+def gather_kernel(
+    sections,
+    me_ref,
+    normed_ref,
+    part_ref,
+    own_ref,
+    far_ref,
+    early_ref,
+    wkv_ref,
+    out_ref,
+    query_ref,
+    wkv_out_ref,
+    fresh_ref,
+    total,
+    fresh,
+):
+    i = pl.program_id(0)
+    me = me_ref[0]
+    owner = i // TILES
+    k = i % TILES
+    tile = out_ref.shape[0]
+    mine = owner == me
+    fed = jnp.logical_or(
+        jnp.logical_and(me == sections - 1, owner == sections - 2),
+        jnp.logical_and(me == 0, owner == 1),
+    )
+    early = jnp.logical_and(
+        fed, jnp.logical_and(k >= TILES - EARLY - LATE, k < TILES - LATE)
+    )
+    late = jnp.logical_and(fed, k >= TILES - LATE)
+
+    @pl.when(i == 0)
+    def _():
+        total[...] = part_ref[...]
+        fresh[...] = jnp.zeros_like(fresh)
+
+    features = normed_ref[:, pl.ds(pl.multiple_of(i * tile, 128), tile)]
+    wkv_out_ref[...] = wkv_ref[...]
+    fresh[...] += jnp.dot(features, wkv_ref[...], preferred_element_type=jnp.float32)
+
+    def keep(ref):
+        out_ref[...] = ref[...]
+        total[...] += jnp.dot(features, ref[...], preferred_element_type=jnp.float32)
+
+    pl.when(mine)(lambda: keep(own_ref))
+    pl.when(early)(lambda: keep(early_ref))
+    other = jnp.logical_or(mine, jnp.logical_or(early, late))
+    pl.when(jnp.logical_not(other))(lambda: keep(far_ref))
+
+    @pl.when(i == pl.num_programs(0) - 1)
+    def _():
+        query_ref[...] = total[...]
+        fresh_ref[...] = fresh[...]
+
+
+def gather(me, normed, part, wq_old, far, early, wkv, sections):
+    rows, total_depth = normed.shape
+    depth, columns = wq_old.shape
+    tile = depth // TILES
+    width = wkv.shape[1]
+
+    def own_at(i, me):
+        return (jnp.clip(i - me[0] * TILES, 0, TILES - 1), 0)
+
+    def far_at(i, me):
+        own = i // TILES == me[0]
+        return (jnp.where(own, jnp.maximum(me[0] * TILES - 1, 0), i), 0)
+
+    def early_at(i, me):
+        feeder = jnp.where(me[0] == sections - 1, sections - 2, 1)
+        return (jnp.clip(i - feeder * TILES - (TILES - EARLY - LATE), 0, EARLY - 1), 0)
+
+    return pl.pallas_call(
+        functools.partial(gather_kernel, sections),
+        out_shape=(
+            jax.ShapeDtypeStruct((total_depth, columns), wq_old.dtype),
+            jax.ShapeDtypeStruct((rows, columns), jnp.float32),
+            jax.ShapeDtypeStruct(wkv.shape, wkv.dtype),
+            jax.ShapeDtypeStruct((rows, width), jnp.float32),
+        ),
+        grid_spec=pltpu.PrefetchScalarGridSpec(
+            num_scalar_prefetch=1,
+            grid=(sections * TILES,),
+            in_specs=[
+                pl.BlockSpec((rows, total_depth), lambda i, me: (0, 0)),
+                pl.BlockSpec((rows, columns), lambda i, me: (0, 0)),
+                pl.BlockSpec((tile, columns), own_at),
+                pl.BlockSpec((tile, columns), far_at),
+                pl.BlockSpec((tile, columns), early_at),
+                pl.BlockSpec((tile, width), lambda i, me: (i, 0)),
+            ],
+            out_specs=(
+                pl.BlockSpec((tile, columns), lambda i, me: (i, 0)),
+                pl.BlockSpec((rows, columns), lambda i, me: (0, 0)),
+                pl.BlockSpec((tile, width), lambda i, me: (i, 0)),
+                pl.BlockSpec((rows, width), lambda i, me: (0, 0)),
+            ),
+            scratch_shapes=[
+                pltpu.VMEM((rows, columns), jnp.float32),
+                pltpu.VMEM((rows, width), jnp.float32),
+            ],
+        ),
+        cost_estimate=pl.CostEstimate(
+            flops=2 * rows * total_depth * columns,
+            bytes_accessed=4 * total_depth * columns,
+            transcendentals=0,
+        ),
+        compiler_params=pltpu.CompilerParams(vmem_limit_bytes=40 * 2**20),
+        name="gather_query",
+    )(me, normed, part, wq_old, far, early, wkv)
+
+
+def place_kernel(sections, depth, late_ref, held_ref, out_ref, buffer, into, out):
+    me = lax.axis_index("section")
+    pieces = into.shape[0]
+    piece = late_ref.shape[0] // pieces
+    feeder = jnp.where(me == 0, 1, sections - 2)
+    start = feeder * depth + depth - late_ref.shape[0]
+
+    def read(p):
+        span = pl.ds(p * piece, piece)
+        return pltpu.make_async_copy(late_ref.at[span, :], buffer.at[span, :], into.at[p])
+
+    def write(p):
+        return pltpu.make_async_copy(
+            buffer.at[pl.ds(p * piece, piece), :],
+            out_ref.at[pl.ds(pl.multiple_of(start + p * piece, 16), piece), :],
+            out.at[p],
+        )
+
+    @pl.when(jnp.logical_or(me == 0, me == sections - 1))
+    def _():
+        for p in range(pieces):
+            read(p).start()
+        for p in range(pieces):
+            read(p).wait()
+            write(p).start()
+        for p in range(pieces):
+            write(p).wait()
+
+
+def place_late(late, wq_new, sections):
+    depth = wq_new.shape[0] // sections
+    pieces = 4
+    hbm = pl.BlockSpec(memory_space=pl.ANY)
+    dma = pltpu.SemaphoreType.DMA
+    return pl.pallas_call(
+        functools.partial(place_kernel, sections, depth),
+        out_shape=jax.ShapeDtypeStruct(wq_new.shape, wq_new.dtype),
+        in_specs=[hbm, hbm],
+        out_specs=hbm,
+        scratch_shapes=[pltpu.VMEM(late.shape, late.dtype), dma((pieces,)), dma((pieces,))],
+        input_output_aliases={1: 0},
+        cost_estimate=pl.CostEstimate(
+            flops=1024, bytes_accessed=4 * late.size, transcendentals=0
+        ),
+        name="place_late",
+    )(late, wq_new)
 
 
 def attend_kernel(
@@ -456,7 +678,7 @@
     )(place.reshape(-1), lengths, arrived, fresh[:, None, :], query)
 
 
-def shards(hidden_state, norm_gain, wq_old, wkv_old, kv_old, page_table, lengths):
+def work(hidden_state, norm_gain, wq_old, wkv_old, kv_old, page_table, lengths):
     sections = lax.axis_size("section")
     tensors = lax.axis_size("tensor")
     section_id = lax.axis_index("section")
@@ -481,19 +703,30 @@
     picks = (mine[:, :, None] & wanted).astype(jnp.int32)
     spots = jnp.sum(picks * (page_table % pool_dev)[:, :, None], axis=1)
     pages = pick_pages(kv_old, spots.reshape(-1), sections)
-    query, arrived, wkv_new, wq_new, _, _ = exchange(
+    depth = wq_old.shape[0]
+    ends = sorted({(sections - 2, sections - 1), (1, 0)})
+    early_rows = depth // TILES * EARLY
+    late_rows = depth // TILES * LATE
+    stop = depth - late_rows
+    early = lax.ppermute(wq_old[stop - early_rows : stop], "section", ends)
+    part, arrived, wkv_far, far, _, _, late = exchange(
         normed, wq_old, pages, wkv_old, sections, tensors, repeats
+    )
+    late = lax.ppermute(late, "section", ends)
+    me = jnp.full((1,), section_id, jnp.int32)
+    wq_new, query, wkv_new, fresh = gather(
+        me, normed, part, wq_old, far, early, wkv_far, sections
     )
     arrived = arrived.reshape(tensors, rows, per_block, page, width)
     place = lax.dynamic_slice_in_dim(owner * per_block + ranks, section_id * rows, rows, 0)
     my_lengths = lax.dynamic_slice_in_dim(lengths, section_id * rows, rows, 0)
-    fresh = jnp.dot(normed, wkv_new, preferred_element_type=jnp.float32)
     fresh_key = rotate(fresh[:, None, :head_dim], my_lengths, head_dim)[:, 0]
     fresh = jnp.concatenate([fresh_key, fresh[:, head_dim:]], axis=1).astype(jnp.bfloat16)
     query = rotate(query.reshape(rows, queries_here, head_dim), my_lengths, head_dim).astype(
         jnp.bfloat16
     )
     cache, context = attend(arrived, place, my_lengths, fresh, query, head_dim)
+    wq_new = place_late(late, wq_new, sections)
     return (context.reshape(rows, queries_here * head_dim), cache[:, None], wq_new, wkv_new)
 
 
@@ -508,7 +741,7 @@
         P(),
     )
     return jax.shard_map(
-        shards,
+        work,
         mesh=mesh,
         in_specs=placed,
         out_specs=(

time: 549 us -> 583 us (1.062)
  waiting for transfers between devices: 0 us -> 63.6 us
  Pallas kernels: 515 us -> 492 us
  local copies, waits for them, and re-layouts: 24.5 us -> 14.6 us
    ppermute x0 -> x2, waiting for transfers between devices: none -> 63.6 us  [the longest x1 63.6 us: work(): early = lax.ppermute(wq_old[stop - early_rows:stop], 'section', ends)]
    pallas_call x1, Pallas kernels: 492 us -> 441 us  [exchange(): pl.pallas_call(functools.partial(exchange_kernel, sections, tensors, loca...]
    pallas_call x0 -> x2, Pallas kernels: none -> 28.7 us  [the longest x1 26.3 us: gather(): pl.pallas_call(functools.partial(gather_kernel, sections), out_shape=(jax...]
    unnamed x13 -> x17, local copies, waits for them, and re-layouts: 24.2 us -> 11.3 us
  transfers between devices with their start and end apart: 0 -> 2, of which waited for: 0 -> 1; matrix products, arithmetic and copies ran while one was open for 0% -> 1% of each run, Pallas kernels for 0% -> 7%
where the time goes in v1:
time: 583 us; the launch traced here: 582 us
  Pallas kernels  492 us (84%)
  waiting for transfers between devices  63.6 us (11%)
  local copies, waits for them, and re-layouts  14.6 us (3%)
  other arithmetic  8.19 us (1%)
    pallas_call x1, Pallas kernels, exchange(): pl.pallas_call(functools.partial(exchange_kernel, sections, tensors, loca...  441 us
    ppermute x1, waiting for transfers between devices, work(): early = lax.ppermute(wq_old[stop - early_rows:stop], 'section', ends)  63.6 us
    pallas_call x1, Pallas kernels, gather(): pl.pallas_call(functools.partial(gather_kernel, sections), out_shape=(jax...  26.3 us
    pallas_call x1, Pallas kernels, attend(): pl.pallas_call(functools.partial(attend_kernel, pages_of, per_block, page...  15.9 us
  transfers between devices with their start and end apart: 2, of which 1 were waited for; matrix products, arithmetic and copies ran while one was open for 1% of the time, Pallas kernels for 7%

profile of v1, /device:TPU:0, one launch (start us, length us, event | category | flops | bytes accessed | tf_op | source)
XLA Modules:
  0.0 582.1 jit_solution(11625717818235792658)
XLA Ops:
  0.6 0.8 copy.36
  1.5 2.3 select_reduce_fusion.1
  3.8 1.1 fusion.4
  4.9 2.2 select_reduce_fusion
  7.1 0.1 reshape.171.spots_ref
  7.2 1.1 fusion.6.normed_ref
  8.3 6.7 %pick_pages.1.pages_ref = bf16[4,2,128,16,256]{4,3,2,1,0:T(8,128)(2,1)S(1)} custom-call(s32[512]{0:T(512)S(1)} %reshape.171.spots_ref, bf16[2,512,16,256]{3,2,1,0:T(8,128)(2,1)} %kv_ref.1), custom_call_target="tpu_custom_call" | custom-call | tf_op jit(solution)/shard_map/pick_pages/pallas_call | solution.py:50
  15.1 0.0 copy-start
  15.1 3.4 copy-done
  18.5 440.9 %exchange.1 = (f32[16,1024]{1,0:T(8,128)S(1)}, bf16[8,128,16,256]{3,2,1,0:T(8,128)(2,1)}, bf16[8192,256]{1,0:T(8,128)(2,1)S(1)}, bf16[8192,1024]{1,0:T(8,128)(2,...) custom-call(bf16[16,8192]{1,0:T(8,128)(2,1)S(1)} %fusion.6.normed_ref, ...), custom_call_target="tpu_custom_call" | custom-call | flops 67108864 | bytes 419430400 | tf_op jit(solution)/shard_map/exchange/pallas_call | solution.py:403
  459.4 2.0 copy-done.3
  461.4 1.4 collective-permute-start.1
  462.8 2.3 slice.22
  465.1 1.3 collective-permute-start
  466.4 0.7 dynamic-slice_add_fusion
  467.1 0.8 copy.40
  467.9 0.1 reshape.170.place_ref
  468.0 0.0 copy-done.6
  468.0 0.1 fusion.10
  468.1 0.1 multiply_cosine_fusion
  468.2 63.6 %collective-permute-done.early_ref = bf16[512,1024]{1,0:T(8,128)(2,1)S(1)} collective-permute-done((bf16[512,1024]{1,0:T(8,128)(2,1)}, bf16[512,1024]{1,0:T(8,128)(2,1)S(1)}, u32[]{:S(2)}, u32[]{:S(2)}) %collective-permute-start) | collective-permute-done | bytes 1048608 | tf_op jit(solution)/shard_map/ppermute | solution.py:711
  531.8 2.2 copy-done.1
  534.0 2.2 copy-done.4
  536.2 26.3 %gather_query.1 = (bf16[8192,1024]{1,0:T(8,128)(2,1)}, f32[16,1024]{1,0:T(8,128)S(1)}, bf16[8192,256]{1,0:T(8,128)(2,1)}, f32[16,256]{1,0:T(8,128)S(1)}) custom-call(s32[1]{0:T(128)} %bitcast.1.me_ref, bf16[16,8192]{1,0:T(8,128)(2,1)S(1)} %fusion.6.normed_ref, f32[16,1024]{1,0:T(8,128)S(1)} %get-tuple-element.16.part_ref, bf16[2048,1024]{1,0:T(8,128)(2,1)S(1)} %copy-done.1, ...), custom_call_target="tpu_custom_call" | custom-call | flops 268435456 | bytes 33554432 | tf_op jit(solution)/shard_map/gather_query/pallas_call | solution.py:523
  562.5 0.1 mul.133
  562.6 0.3 subtract_convert_fusion.1
  562.8 0.1 pad_maximum_fusion.1.fresh_ref
  562.9 0.1 subtract_convert_fusion
  563.0 0.1 pad_maximum_fusion.query_ref
  563.1 15.9 %attend.1 = (bf16[16,1024,256]{2,1,0:T(8,128)(2,1)}, bf16[16,8,128]{2,1,0:T(8,128)(2,1)S(1)}) custom-call(s32[1024]{0:T(1024)S(1)} %reshape.170.place_ref, s32[16]{0:T(128)S(1)} %get-tuple-element.47.length_ref, bf16[8,16,8,16,256]{4,3,2,1,0:T(8,128)(2,1)S(1)} %bitcast.15, bf16[16,1,256]{2,1,0:T(2,128)(2,1)S(1)} %pad_maximum_fusion.1.fresh_ref, ...), custom_call_target="tpu_custom_call" | custom-call | flops 67108864 | bytes 16777216 | tf_op jit(solution)/shard_map/attend/pallas_call | solution.py:652
  579.0 0.6 copy.47
  579.7 2.4 place_late.1
  (17 shorter events, 0.1 us)
Async XLA Ops:
  8.3 10.1 %copy-start.5 = (bf16[1024,512]{1,0:T(8,128)(2,1)S(1)}, bf16[1024,512]{1,0:T(8,128)(2,1)}, u32[]{:S(2)}) copy-start(bf16[1024,512]{1,0:T(8,128)(2,1)} %wkv_ref.1) | copy-start | bytes 3145732
  15.1 3.4 copy-start
  459.4 2.0 copy-start.3
  461.4 6.6 %copy-start.6 = (s32[64]{0:T(128)S(1)}, s32[64]{0:T(128)}, u32[]{:S(2)}) copy-start(s32[64]{0:T(128)} %param.13) | copy-start | bytes 772
  461.4 118.3 %collective-permute-start.1 = (bf16[1024,1024]{1,0:T(8,128)(2,1)S(1)}, bf16[1024,1024]{1,0:T(8,128)(2,1)}, u32[]{:S(2)}, u32[]{:S(2)}) collective-permute-start(bf16[1024,1024]{1,0:T(8,128)(2,1)S(1)} %get-tuple-element.23), channel_id=1, source_target_pairs={{8,0},{16,24},{9,1},{17,25},{10,2},{18,26},{11,3},{19,27},{12,4},{... | collective-permute-start | bytes 6291464 | tf_op jit(solution)/shard_map/ppermute | solution.py:715
  465.1 66.7 %collective-permute-start = (bf16[512,1024]{1,0:T(8,128)(2,1)}, bf16[512,1024]{1,0:T(8,128)(2,1)S(1)}, u32[]{:S(2)}, u32[]{:S(2)}) collective-permute-start(bf16[512,1024]{1,0:T(8,128)(2,1)} %slice.22), channel_id=1, source_target_pairs={{8,0},{16,24},{9,1},{17,25},{10,2},{18,26},{11,3},{19,27},{12,4},{... | collective-permute-start | bytes 3145736 | tf_op jit(solution)/shard_map/ppermute | solution.py:711
  531.8 2.2 copy-start.1
  534.0 2.2 copy-start.4
  536.2 26.9 %copy-start.2 = (bf16[8,128,16,256]{3,2,1,0:T(8,128)(2,1)S(1)}, bf16[8,128,16,256]{3,2,1,0:T(8,128)(2,1)}, u32[]{:S(2)}) copy-start(bf16[8,128,16,256]{3,2,1,0:T(8,128)(2,1)} %get-tuple-element.15) | copy-start | bytes 25165828

commit v2 on v1

--- a/solution.py
+++ b/solution.py
@@ -15,10 +15,19 @@
 EPSILON = 1e-05
 ROPE_BASE = 500000.0
 MESH = pl.DeviceIdType.MESH
-CHUNKS = 8
-TILES = 8
-EARLY = 2
-LATE = 4
+CHUNKS = 16
+PIECES = 4
+UNIT = 128
+EARLY = 4
+LATE = 6
+PAIR = 8
+TOGETHER = 4
+VMEM_LIMIT = 60 * 2**20
+
+
+def split(depth):
+    tiles = depth // UNIT
+    return tiles, max(1, tiles * EARLY // 16), max(1, tiles * LATE // 16)
 
 
 def rotate(values, position, head_dim):
@@ -58,7 +67,7 @@
                 (1, 1, count, page, width), lambda h, s, spots: (s, h, 0, 0, 0)
             ),
         ),
-        compiler_params=pltpu.CompilerParams(vmem_limit_bytes=40 * 2**20),
+        compiler_params=pltpu.CompilerParams(vmem_limit_bytes=VMEM_LIMIT),
         name="pick_pages",
     )(spots, kv_old)
 
@@ -169,22 +178,25 @@
             device_id_type=MESH,
         )
 
-    def wkv_own_copy(side):
+    part_rows = block // PIECES
+
+    def wkv_own_copy(side, p):
         return pltpu.make_async_remote_copy(
-            wkv_ref,
-            stage_wkv_ref.at[me],
-            wkv_own_send.at[side],
-            wkv_stage_recv.at[me],
+            wkv_ref.at[pl.ds(p * part_rows, part_rows), :],
+            stage_wkv_ref.at[me, pl.ds(p * part_rows, part_rows), :],
+            wkv_own_send.at[side, p],
+            wkv_stage_recv.at[me, p],
             device_id=(next_to[side], mine),
             device_id_type=MESH,
         )
 
-    def wkv_relay_copy(owner, side):
+    def wkv_relay_copy(owner, side, p):
+        here = stage_wkv_ref.at[owner, pl.ds(p * part_rows, part_rows), :]
         return pltpu.make_async_remote_copy(
-            stage_wkv_ref.at[owner],
-            stage_wkv_ref.at[owner],
-            wkv_relay_send.at[owner],
-            wkv_stage_recv.at[owner],
+            here,
+            here,
+            wkv_relay_send.at[owner, p],
+            wkv_stage_recv.at[owner, p],
             device_id=(next_to[side], mine),
             device_id_type=MESH,
         )
@@ -251,11 +263,13 @@
         )
 
     for side in range(2):
-        pl.when(onward[side])(lambda: wkv_own_copy(side).start())
+        for p in range(PIECES):
+            pl.when(onward[side])(lambda: wkv_own_copy(side, p).start())
         pl.when(fed[side])(lambda: spread_copy(side).start())
     begin(wkv_copy, 0)
     begin(page_copy, 0)
-    each_chunk(send_own)
+    ahead = min(kept, CHUNKS * 3 // 8)
+    each_chunk(send_own, 0, ahead)
     for step in range(sections - 1, 0, -1):
         for side in range(2):
             pl.when(real(side, step))(
@@ -263,6 +277,7 @@
                     me, owner_of(side, step), step if side else sections - step
                 ).start()
             )
+    each_chunk(send_own, ahead)
 
     take = pltpu.make_async_copy(
         wq_ref.at[pl.ds(depth - late_rows, late_rows), :], held, local_sem.at[2]
@@ -289,16 +304,21 @@
             part_copy(side).start()
 
     def pass_wkv(step):
+        for p in range(PIECES):
+            for side in range(2):
+                owner = owner_of(side, step)
+
+                @pl.when(real(side, step))
+                def _():
+                    wkv_relay_copy(owner, side, p).wait_recv()
+                    pl.when(onward[side])(lambda: wkv_relay_copy(owner, side, p).start())
+
         for side in range(2):
-            owner = owner_of(side, step)
-
-            @pl.when(real(side, step))
-            def _():
-                wkv_relay_copy(owner, side).wait_recv()
-                pl.when(onward[side])(lambda: wkv_relay_copy(owner, side).start())
-                begin(wkv_copy, step if side else sections - step)
-
-    def pass_wq(step):
+            pl.when(real(side, step))(
+                lambda: begin(wkv_copy, step if side else sections - step)
+            )
+
+    def pass_wq(step, first=0, stop=chunks):
         def pass_on(i):
             for side in range(2):
                 owner = owner_of(side, step)
@@ -313,16 +333,26 @@
                     relay_copy(owner, side, i).wait_recv()
                     pl.when(onward[side])(lambda: relay_copy(owner, side, i).start())
 
-        each_chunk(pass_on)
-
-    for step in range(1, sections):
+        each_chunk(pass_on, first, stop)
+
+    def spread_pages(away, other):
+        stage_copy(other, other, away).wait_recv()
+        begin(page_copy, away)
+
+    pass_wkv(1)
+    pass_wq(1, 0, ahead)
+    for step in range(sections - 1, 0, -1):
+        for side in range(2):
+            pl.when(real(side, step))(
+                lambda: spread_pages(
+                    step if side else sections - step, owner_of(side, step)
+                )
+            )
+    pass_wq(1, ahead)
+    for step in range(2, sections):
         pass_wkv(step)
-        pass_wq(step)
-        if step == 1:
-            for away in range(1, sections):
-                other = lax.rem(me + away, sections)
-                stage_copy(other, other, away).wait_recv()
-                begin(page_copy, away)
+        if step < last:
+            pass_wq(step)
 
     put.wait()
     for side in range(2):
@@ -353,11 +383,12 @@
 
     each_chunk(sent)
     for side in range(2):
-        pl.when(onward[side])(lambda: wkv_own_copy(side).wait_send())
-        for step in range(1, sections):
-            pl.when(jnp.logical_and(real(side, step), onward[side]))(
-                lambda: wkv_relay_copy(owner_of(side, step), side).wait_send()
-            )
+        for p in range(PIECES):
+            pl.when(onward[side])(lambda: wkv_own_copy(side, p).wait_send())
+            for step in range(1, sections):
+                pl.when(jnp.logical_and(real(side, step), onward[side]))(
+                    lambda: wkv_relay_copy(owner_of(side, step), side, p).wait_send()
+                )
     for step in range(1, sections):
         stage_copy(me, lax.rem(me + step, sections), step).wait_send()
     for make in (page_copy, wkv_copy):
@@ -387,6 +418,8 @@
         outside = mine != origin
         pl.when(outside)(pages_in.wait_recv)
         pl.when(outside)(wkv_in.wait_recv)
+    if last > 1:
+        pass_wq(last)
 
 
 def exchange(normed, wq_old, pages, wkv_old, sections, tensors, repeats):
@@ -395,8 +428,9 @@
     local_heads = pages.shape[1]
     width = pages.shape[4]
     copies = sections * local_heads * repeats
-    late_rows = depth // TILES * LATE
-    kept = CHUNKS // TILES * (TILES - EARLY - LATE)
+    tiles, early, late = split(depth)
+    late_rows = late * UNIT
+    kept = (tiles - early - late) * UNIT * CHUNKS // depth
     dma = pltpu.SemaphoreType.DMA
     vmem = pl.BlockSpec(memory_space=pltpu.VMEM)
     hbm = pl.BlockSpec(memory_space=pl.ANY)
@@ -430,14 +464,14 @@
             dma((sections, CHUNKS)),
             dma((sections,)),
             dma((sections,)),
-            dma((2,)),
-            dma((sections,)),
-            dma((sections,)),
+            dma((2, PIECES)),
+            dma((sections, PIECES)),
+            dma((sections, PIECES)),
             dma((3,)),
             dma((3,)),
         ],
         compiler_params=pltpu.CompilerParams(
-            has_side_effects=True, vmem_limit_bytes=40 * 2**20
+            has_side_effects=True, vmem_limit_bytes=VMEM_LIMIT
         ),
         cost_estimate=pl.CostEstimate(
             flops=4 * rows * late_rows * columns,
@@ -450,6 +484,10 @@
 
 def gather_kernel(
     sections,
+    tiles,
+    first,
+    last,
+    pair,
     me_ref,
     normed_ref,
     part_ref,
@@ -466,36 +504,44 @@
 ):
     i = pl.program_id(0)
     me = me_ref[0]
-    owner = i // TILES
-    k = i % TILES
-    tile = out_ref.shape[0]
+    owner = i // (tiles // pair)
+    tile = UNIT
     mine = owner == me
     fed = jnp.logical_or(
         jnp.logical_and(me == sections - 1, owner == sections - 2),
         jnp.logical_and(me == 0, owner == 1),
     )
-    early = jnp.logical_and(
-        fed, jnp.logical_and(k >= TILES - EARLY - LATE, k < TILES - LATE)
-    )
-    late = jnp.logical_and(fed, k >= TILES - LATE)
 
     @pl.when(i == 0)
     def _():
         total[...] = part_ref[...]
         fresh[...] = jnp.zeros_like(fresh)
 
-    features = normed_ref[:, pl.ds(pl.multiple_of(i * tile, 128), tile)]
+    def keep(ref, rows, at):
+        out_ref[pl.ds(at * tile, tile), :] = ref[rows, :]
+
+    for at in range(pair):
+        k = (i % (tiles // pair)) * pair + at
+        rows = pl.ds(at * tile, tile)
+        early = jnp.logical_and(fed, jnp.logical_and(k >= first, k < last))
+        late = jnp.logical_and(fed, k >= last)
+        start = jnp.clip(k - first, 0, last - first - 1) * tile
+        other = jnp.logical_or(mine, jnp.logical_or(early, late))
+        pl.when(mine)(lambda: keep(own_ref, rows, at))
+        pl.when(early)(
+            lambda: keep(early_ref, pl.ds(pl.multiple_of(start, UNIT), tile), at)
+        )
+        pl.when(jnp.logical_not(other))(lambda: keep(far_ref, rows, at))
+
+        @pl.when(late)
+        def _():
+            out_ref[rows, :] = jnp.zeros((tile, out_ref.shape[1]), out_ref.dtype)
+
+    span = pl.ds(pl.multiple_of(i * pair * tile, UNIT), pair * tile)
+    features = normed_ref[:, span]
+    total[...] += jnp.dot(features, out_ref[...], preferred_element_type=jnp.float32)
     wkv_out_ref[...] = wkv_ref[...]
     fresh[...] += jnp.dot(features, wkv_ref[...], preferred_element_type=jnp.float32)
-
-    def keep(ref):
-        out_ref[...] = ref[...]
-        total[...] += jnp.dot(features, ref[...], preferred_element_type=jnp.float32)
-
-    pl.when(mine)(lambda: keep(own_ref))
-    pl.when(early)(lambda: keep(early_ref))
-    other = jnp.logical_or(mine, jnp.logical_or(early, late))
-    pl.when(jnp.logical_not(other))(lambda: keep(far_ref))
 
     @pl.when(i == pl.num_programs(0) - 1)
     def _():
@@ -506,22 +552,28 @@
 def gather(me, normed, part, wq_old, far, early, wkv, sections):
     rows, total_depth = normed.shape
     depth, columns = wq_old.shape
-    tile = depth // TILES
+    tiles, early_tiles, late_tiles = split(depth)
+    pair = min(PAIR, tiles)
+    steps = tiles // pair
+    tile = pair * UNIT
     width = wkv.shape[1]
 
     def own_at(i, me):
-        return (jnp.clip(i - me[0] * TILES, 0, TILES - 1), 0)
+        return (jnp.clip(i - me[0] * steps, 0, steps - 1), 0)
 
     def far_at(i, me):
-        own = i // TILES == me[0]
-        return (jnp.where(own, jnp.maximum(me[0] * TILES - 1, 0), i), 0)
-
-    def early_at(i, me):
-        feeder = jnp.where(me[0] == sections - 1, sections - 2, 1)
-        return (jnp.clip(i - feeder * TILES - (TILES - EARLY - LATE), 0, EARLY - 1), 0)
+        own = i // steps == me[0]
+        return (jnp.where(own, jnp.maximum(me[0] * steps - 1, 0), i), 0)
 
     return pl.pallas_call(
-        functools.partial(gather_kernel, sections),
+        functools.partial(
+            gather_kernel,
+            sections,
+            tiles,
+            tiles - early_tiles - late_tiles,
+            tiles - late_tiles,
+            pair,
+        ),
         out_shape=(
             jax.ShapeDtypeStruct((total_depth, columns), wq_old.dtype),
             jax.ShapeDtypeStruct((rows, columns), jnp.float32),
@@ -530,13 +582,13 @@
         ),
         grid_spec=pltpu.PrefetchScalarGridSpec(
             num_scalar_prefetch=1,
-            grid=(sections * TILES,),
+            grid=(sections * steps,),
             in_specs=[
                 pl.BlockSpec((rows, total_depth), lambda i, me: (0, 0)),
                 pl.BlockSpec((rows, columns), lambda i, me: (0, 0)),
                 pl.BlockSpec((tile, columns), own_at),
                 pl.BlockSpec((tile, columns), far_at),
-                pl.BlockSpec((tile, columns), early_at),
+                pl.BlockSpec(early.shape, lambda i, me: (0, 0)),
                 pl.BlockSpec((tile, width), lambda i, me: (i, 0)),
             ],
             out_specs=(
@@ -555,35 +607,28 @@
             bytes_accessed=4 * total_depth * columns,
             transcendentals=0,
         ),
-        compiler_params=pltpu.CompilerParams(vmem_limit_bytes=40 * 2**20),
+        compiler_params=pltpu.CompilerParams(vmem_limit_bytes=VMEM_LIMIT),
         name="gather_query",
     )(me, normed, part, wq_old, far, early, wkv)
 
 
-def place_kernel(sections, depth, late_ref, held_ref, out_ref, buffer, into, out):
+def place_kernel(sections, depth, late_ref, held_ref, out_ref, done):
     me = lax.axis_index("section")
-    pieces = into.shape[0]
+    pieces = done.shape[0]
     piece = late_ref.shape[0] // pieces
     feeder = jnp.where(me == 0, 1, sections - 2)
     start = feeder * depth + depth - late_ref.shape[0]
 
-    def read(p):
-        span = pl.ds(p * piece, piece)
-        return pltpu.make_async_copy(late_ref.at[span, :], buffer.at[span, :], into.at[p])
-
     def write(p):
         return pltpu.make_async_copy(
-            buffer.at[pl.ds(p * piece, piece), :],
+            late_ref.at[pl.ds(p * piece, piece), :],
             out_ref.at[pl.ds(pl.multiple_of(start + p * piece, 16), piece), :],
-            out.at[p],
+            done.at[p],
         )
 
     @pl.when(jnp.logical_or(me == 0, me == sections - 1))
     def _():
         for p in range(pieces):
-            read(p).start()
-        for p in range(pieces):
-            read(p).wait()
             write(p).start()
         for p in range(pieces):
             write(p).wait()
@@ -591,91 +636,131 @@
 
 def place_late(late, wq_new, sections):
     depth = wq_new.shape[0] // sections
-    pieces = 4
     hbm = pl.BlockSpec(memory_space=pl.ANY)
-    dma = pltpu.SemaphoreType.DMA
     return pl.pallas_call(
         functools.partial(place_kernel, sections, depth),
         out_shape=jax.ShapeDtypeStruct(wq_new.shape, wq_new.dtype),
-        in_specs=[hbm, hbm],
+        in_specs=[pl.BlockSpec(memory_space=pltpu.VMEM), hbm],
         out_specs=hbm,
-        scratch_shapes=[pltpu.VMEM(late.shape, late.dtype), dma((pieces,)), dma((pieces,))],
+        scratch_shapes=[pltpu.SemaphoreType.DMA((2,))],
         input_output_aliases={1: 0},
         cost_estimate=pl.CostEstimate(
             flops=1024, bytes_accessed=4 * late.size, transcendentals=0
         ),
+        compiler_params=pltpu.CompilerParams(vmem_limit_bytes=16 * 2**20),
         name="place_late",
     )(late, wq_new)
 
 
+def take_kernel(start, from_ref, out_ref, done):
+    copy = pltpu.make_async_copy(from_ref.at[pl.ds(start, out_ref.shape[0]), :], out_ref, done)
+    copy.start()
+    copy.wait()
+
+
+def take_rows(array, start, rows):
+    return pl.pallas_call(
+        functools.partial(take_kernel, start),
+        out_shape=jax.ShapeDtypeStruct((rows, array.shape[1]), array.dtype),
+        in_specs=[pl.BlockSpec(memory_space=pl.ANY)],
+        out_specs=pl.BlockSpec(memory_space=pltpu.VMEM),
+        scratch_shapes=[pltpu.SemaphoreType.DMA],
+        compiler_params=pltpu.CompilerParams(vmem_limit_bytes=VMEM_LIMIT),
+        name="take_rows",
+    )(array)
+
+
 def attend_kernel(
-    pages_of, per_block, page, head_dim, place_ref, length_ref, in_ref, fresh_ref, query_ref, cache_ref, context_ref
+    pages_of, together, page, head_dim, block_ref, spot_ref, length_ref, in_ref, fresh_ref, query_ref, cache_ref, context_ref, mixed
 ):
-    request = pl.program_id(0)
-    length = length_ref[request]
-    base = request * pages_of
+    step = pl.program_id(0)
 
     def order(j, carry):
-        spot = place_ref[base + j]
         start = pl.multiple_of(j * page, page)
-        cache_ref[0, pl.ds(start, page), :] = in_ref[
-            lax.div(spot, per_block), 0, lax.rem(spot, per_block)
-        ]
+        for r in range(together):
+            at = (step * together + r) * pages_of + j
+            cache_ref[r, pl.ds(start, page), :] = in_ref[block_ref[at], r, spot_ref[at]]
         return carry
 
     lax.fori_loop(0, pages_of, order, 0, unroll=8)
-    start = pl.multiple_of(lax.div(length, page) * page, page)
-    held = cache_ref[0, pl.ds(start, page), :]
-    row = lax.broadcasted_iota(jnp.int32, held.shape, 0)
-    fresh = jnp.broadcast_to(fresh_ref[0].astype(jnp.float32), held.shape)
-    cache_ref[0, pl.ds(start, page), :] = jnp.where(
-        row == lax.rem(length, page), fresh, held.astype(jnp.float32)
-    ).astype(held.dtype)
-    keys = cache_ref[0, :, :head_dim]
-    values = cache_ref[0, :, head_dim:]
-    scores = lax.dot_general(
-        query_ref[0], keys, (((1,), (1,)), ((), ())), preferred_element_type=jnp.float32
-    ) * head_dim ** (-0.5)
-    seen = lax.broadcasted_iota(jnp.int32, scores.shape, 1) <= length
-    peak = jnp.max(jnp.where(seen, scores, -jnp.inf), axis=1, keepdims=True)
-    weights = jnp.where(seen, jnp.exp(scores - peak), 0.0)
-    probs = (weights / jnp.sum(weights, axis=1, keepdims=True)).astype(jnp.bfloat16)
-    context_ref[0] = jnp.dot(probs, values, preferred_element_type=jnp.float32).astype(
-        context_ref.dtype
-    )
-
-
-def attend(arrived, place, lengths, fresh, query, head_dim):
+    for r in range(together):
+        length = length_ref[step * together + r]
+        start = pl.multiple_of(lax.div(length, page) * page, page)
+        held = cache_ref[r, pl.ds(start, page), :]
+        row = lax.broadcasted_iota(jnp.int32, held.shape, 0)
+        fresh = jnp.broadcast_to(fresh_ref[r].astype(jnp.float32), held.shape)
+        cache_ref[r, pl.ds(start, page), :] = jnp.where(
+            row == lax.rem(length, page), fresh, held.astype(jnp.float32)
+        ).astype(held.dtype)
+    scores = [
+        lax.dot_general(
+            query_ref[r],
+            cache_ref[r, :, :head_dim],
+            (((1,), (1,)), ((), ())),
+            preferred_element_type=jnp.float32,
+        )
+        * head_dim ** (-0.5)
+        for r in range(together)
+    ]
+    seen = [
+        lax.broadcasted_iota(jnp.int32, scores[r].shape, 1) <= length_ref[step * together + r]
+        for r in range(together)
+    ]
+    peak = [
+        jnp.max(jnp.where(seen[r], scores[r], -jnp.inf), axis=1, keepdims=True)
+        for r in range(together)
+    ]
+    weights = [jnp.where(seen[r], jnp.exp(scores[r] - peak[r]), 0.0) for r in range(together)]
+    sums = [jnp.sum(weights[r], axis=1, keepdims=True) for r in range(together)]
+    probs = [(weights[r] / sums[r]).astype(jnp.bfloat16) for r in range(together)]
+    for r in range(together):
+        mixed[step * together + r] = jnp.dot(
+            probs[r], cache_ref[r, :, head_dim:], preferred_element_type=jnp.float32
+        )
+
+    @pl.when(step == pl.num_programs(0) - 1)
+    def _():
+        for head in range(mixed.shape[1]):
+            context_ref[:, pl.ds(head * head_dim, head_dim)] = mixed[:, head].astype(
+                context_ref.dtype
+            )
+
+
+def attend(arrived, block, spot, lengths, fresh, query, head_dim):
     blocks, rows, per_block, page, width = arrived.shape
     pages_of = blocks * per_block
     heads = query.shape[1]
+    together = next(n for n in (TOGETHER, 2, 1) if rows % n == 0)
     return pl.pallas_call(
-        functools.partial(attend_kernel, pages_of, per_block, page, head_dim),
+        functools.partial(attend_kernel, pages_of, together, page, head_dim),
         out_shape=(
             jax.ShapeDtypeStruct((rows, pages_of * page, width), arrived.dtype),
-            jax.ShapeDtypeStruct(query.shape, jnp.bfloat16),
+            jax.ShapeDtypeStruct((rows, heads * head_dim), jnp.bfloat16),
         ),
         grid_spec=pltpu.PrefetchScalarGridSpec(
-            num_scalar_prefetch=2,
-            grid=(rows,),
+            num_scalar_prefetch=3,
+            grid=(rows // together,),
             in_specs=[
-                pl.BlockSpec((blocks, 1, per_block, page, width), lambda r, *_: (0, r, 0, 0, 0)),
-                pl.BlockSpec((1, 1, width), lambda r, *_: (r, 0, 0)),
-                pl.BlockSpec((1, heads, head_dim), lambda r, *_: (r, 0, 0)),
+                pl.BlockSpec(
+                    (blocks, together, per_block, page, width), lambda r, *_: (0, r, 0, 0, 0)
+                ),
+                pl.BlockSpec((together, 1, width), lambda r, *_: (r, 0, 0)),
+                pl.BlockSpec((together, heads, head_dim), lambda r, *_: (r, 0, 0)),
             ],
             out_specs=(
-                pl.BlockSpec((1, pages_of * page, width), lambda r, *_: (r, 0, 0)),
-                pl.BlockSpec((1, heads, head_dim), lambda r, *_: (r, 0, 0)),
+                pl.BlockSpec((together, pages_of * page, width), lambda r, *_: (r, 0, 0)),
+                pl.BlockSpec((rows, heads * head_dim), lambda r, *_: (0, 0)),
             ),
+            scratch_shapes=[pltpu.VMEM((rows, heads, head_dim), jnp.float32)],
         ),
         cost_estimate=pl.CostEstimate(
             flops=4 * rows * heads * pages_of * page * head_dim,
             bytes_accessed=4 * arrived.size,
             transcendentals=rows * heads * pages_of * page,
         ),
-        compiler_params=pltpu.CompilerParams(vmem_limit_bytes=40 * 2**20),
+        compiler_params=pltpu.CompilerParams(vmem_limit_bytes=VMEM_LIMIT),
         name="attend",
-    )(place.reshape(-1), lengths, arrived, fresh[:, None, :], query)
+    )(block.reshape(-1), spot.reshape(-1), lengths, arrived, fresh[:, None, :], query)
 
 
 def work(hidden_state, norm_gain, wq_old, wkv_old, kv_old, page_table, lengths):
@@ -705,10 +790,11 @@
     pages = pick_pages(kv_old, spots.reshape(-1), sections)
     depth = wq_old.shape[0]
     ends = sorted({(sections - 2, sections - 1), (1, 0)})
-    early_rows = depth // TILES * EARLY
-    late_rows = depth // TILES * LATE
-    stop = depth - late_rows
-    early = lax.ppermute(wq_old[stop - early_rows : stop], "section", ends)
+    tiles, early_tiles, late_tiles = split(depth)
+    early = take_rows(
+        wq_old, (tiles - early_tiles - late_tiles) * UNIT, early_tiles * UNIT
+    )
+    early = lax.ppermute(early, "section", ends)
     part, arrived, wkv_far, far, _, _, late = exchange(
         normed, wq_old, pages, wkv_old, sections, tensors, repeats
     )
@@ -718,16 +804,17 @@
         me, normed, part, wq_old, far, early, wkv_far, sections
     )
     arrived = arrived.reshape(tensors, rows, per_block, page, width)
-    place = lax.dynamic_slice_in_dim(owner * per_block + ranks, section_id * rows, rows, 0)
+    block = lax.dynamic_slice_in_dim(owner, section_id * rows, rows, 0)
+    spot = lax.dynamic_slice_in_dim(ranks, section_id * rows, rows, 0)
     my_lengths = lax.dynamic_slice_in_dim(lengths, section_id * rows, rows, 0)
     fresh_key = rotate(fresh[:, None, :head_dim], my_lengths, head_dim)[:, 0]
     fresh = jnp.concatenate([fresh_key, fresh[:, head_dim:]], axis=1).astype(jnp.bfloat16)
     query = rotate(query.reshape(rows, queries_here, head_dim), my_lengths, head_dim).astype(
         jnp.bfloat16
     )
-    cache, context = attend(arrived, place, my_lengths, fresh, query, head_dim)
+    cache, context = attend(arrived, block, spot, my_lengths, fresh, query, head_dim)
     wq_new = place_late(late, wq_new, sections)
-    return (context.reshape(rows, queries_here * head_dim), cache[:, None], wq_new, wkv_new)
+    return (context, cache[:, None], wq_new, wkv_new)
 
 
 def solution(mesh):

time: 583 us -> 493 us (0.85)
  waiting for transfers between devices: 63.6 us -> 0.01 us
  Pallas kernels: 492 us -> 475 us
  local copies, waits for them, and re-layouts: 14.6 us -> 5.73 us
    ppermute x1, waiting for transfers between devices: 63.6 us -> 0.01 us  [work(): early = lax.ppermute(early, 'section', ends)]
    pallas_call x2 -> x3, Pallas kernels: 42.2 us -> 31.9 us  [the longest x1 18.6 us: gather(): pl.pallas_call(functools.partial(gather_kernel, sections, tiles, tiles -...]
    unnamed x17 -> x11, local copies, waits for them, and re-layouts: 11.3 us -> 1.83 us
    pallas_call x1, Pallas kernels: 441 us -> 432 us  [exchange(): pl.pallas_call(functools.partial(exchange_kernel, sections, tensors, loca...]
  transfers between devices with their start and end apart: 2 -> 2, of which waited for: 1 -> 0; matrix products, arithmetic and copies ran while one was open for 1% -> 3% of each run, Pallas kernels for 7% -> 96%
where the time goes in v2:
time: 493 us
  Pallas kernels  475 us (96%)
  other arithmetic  8.04 us (2%)
  local copies, waits for them, and re-layouts  5.73 us (1%)
    pallas_call x1, Pallas kernels, exchange(): pl.pallas_call(functools.partial(exchange_kernel, sections, tensors, loca...  432 us
    pallas_call x1, Pallas kernels, gather(): pl.pallas_call(functools.partial(gather_kernel, sections, tiles, tiles -...  18.6 us
    pallas_call x1, Pallas kernels, attend(): pl.pallas_call(functools.partial(attend_kernel, pages_of, together, page,...  11 us
    pallas_call x1, Pallas kernels, pick_pages(): pl.pallas_call(functools.partial(pick_kernel, count), out_shape=jax.Shape...  10 us
  transfers between devices with their start and end apart: 2, of which 0 were waited for; matrix products, arithmetic and copies ran while one was open for 3% of the time, Pallas kernels for 96%

profile of v2, /device:TPU:0, one launch (start us, length us, event | category | flops | bytes accessed | tf_op | source)
XLA Modules:
  0.0 492.6 jit_solution(10970083417459160812)
XLA Ops:
  0.7 2.2 take_rows.1
  2.9 1.3 collective-permute-start
  4.3 0.1 copy.28
  4.4 0.2 fusion.4
  4.6 0.1 copy.31
  4.6 0.1 copy.30
  4.8 0.8 fusion.6.normed_ref
  5.6 2.2 select_reduce_fusion.1
  7.9 2.2 select_reduce_fusion
  10.1 0.7 reshape.172.spots_ref
  10.8 10.0 %pick_pages.1.pages_ref = bf16[4,2,128,16,256]{4,3,2,1,0:T(8,128)(2,1)} custom-call(s32[512]{0:T(512)} %reshape.172.spots_ref, bf16[2,512,16,256]{3,2,1,0:T(8,128)(2,1)} %kv_ref.1), custom_call_target="tpu_custom_call" | custom-call | tf_op jit(solution)/shard_map/pick_pages/pallas_call | solution.py:59
  20.8 432.5 %exchange.1 = (f32[16,1024]{1,0:T(8,128)}, bf16[8,128,16,256]{3,2,1,0:T(8,128)(2,1)}, bf16[8192,256]{1,0:T(8,128)(2,1)}, bf16[8192,1024]{1,0:T(8,128)(2,1)}, bf1...) custom-call(bf16[16,8192]{1,0:T(8,128)(2,1)} %fusion.6.normed_ref, ...), custom_call_target="tpu_custom_call" | custom-call | flops 50331648 | bytes 419430400 | tf_op jit(solution)/shard_map/exchange/pallas_call | solution.py:437
  453.2 1.3 collective-permute-start.1
  454.5 0.7 reshape.170.block_ref
  455.2 0.1 constant_dynamic-slice_fusion
  455.3 0.1 copy.29
  455.3 0.7 reshape.171.spot_ref
  456.0 0.6 fusion.10
  456.7 0.1 multiply_cosine_fusion
  456.8 0.0 copy-start
  456.8 1.0 copy-done
  457.8 18.6 %gather_query.1 = (bf16[8192,1024]{1,0:T(8,128)(2,1)}, f32[16,1024]{1,0:T(8,128)}, bf16[8192,256]{1,0:T(8,128)(2,1)}, f32[16,256]{1,0:T(8,128)}) custom-call(s32[1]{0:T(128)} %bitcast.1.me_ref, bf16[16,8192]{1,0:T(8,128)(2,1)} %fusion.6.normed_ref, f32[16,1024]{1,0:T(8,128)} %get-tuple-element.16.part_ref, bf16[2048,1024]{1,0:T(8,128)(2,1)} %own_ref.1, ...), custom_call_target="tpu_custom_call" | custom-call | flops 268435456 | bytes 33554432 | tf_op jit(solution)/shard_map/gather_query/pallas_call | solution.py:568
  476.4 0.7 slice.19
  477.1 0.7 fusion.9
  477.8 0.9 copy.35
  478.7 0.1 mul.126
  478.7 0.3 subtract_convert_fusion.1
  479.0 0.7 pad_maximum_fusion.1.fresh_ref
  479.7 0.1 subtract_convert_fusion
  479.8 0.7 pad_maximum_fusion.query_ref
  480.5 11.0 %attend.1 = (bf16[16,1024,256]{2,1,0:T(8,128)(2,1)}, bf16[16,1024]{1,0:T(8,128)(2,1)}) custom-call(s32[1024]{0:T(1024)} %reshape.170.block_ref, s32[1024]{0:T(1024)} %reshape.171.spot_ref, s32[16]{0:T(128)} %get-tuple-element.43.length_ref, bf16[8,16,8,16,256]{4,3,2,1,0:T(8,128)(2,1)} %bitcast.11, bf16[16,1,256]{2,1,0:T(2,128)(2,1)} %pad_maximum_fusion.1.fresh_ref, ...), custom_call_target="tpu_custom_call" | custom-call | flops 67108864 | bytes 16777216 | tf_op jit(solution)/shard_map/attend/pallas_call | solution.py:734
  491.5 1.2 place_late.1
  (16 shorter events, 0.1 us)
Async XLA Ops:
  0.6 3.6 copy-start.2
  0.6 3.7 copy-start.1
  0.7 4.1 copy-start.3
  2.9 453.9 %collective-permute-start = (bf16[512,1024]{1,0:T(8,128)(2,1)}, bf16[512,1024]{1,0:T(8,128)(2,1)S(1)}, u32[]{:S(2)}, u32[]{:S(2)}) collective-permute-start(bf16[512,1024]{1,0:T(8,128)(2,1)} %take_rows.1), channel_id=1, source_target_pairs={{8,0},{16,24},{9,1},{17,25},{10,2},{18,26},{11,3},{19,27},{12,4},{... | collective-permute-start | bytes 3145736 | tf_op jit(solution)/shard_map/ppermute | solution.py:797
  20.8 435.3 %copy-start.4 = (s32[64]{0:T(128)S(1)}, s32[64]{0:T(128)}, u32[]{:S(2)}) copy-start(s32[64]{0:T(128)} %param.13) | copy-start | bytes 772
  453.2 38.2 %collective-permute-start.1 = (bf16[768,1024]{1,0:T(8,128)(2,1)}, bf16[768,1024]{1,0:T(8,128)(2,1)S(1)}, u32[]{:S(2)}, u32[]{:S(2)}) collective-permute-start(bf16[768,1024]{1,0:T(8,128)(2,1)} %get-tuple-element.23), channel_id=1, source_target_pairs={{8,0},{16,24},{9,1},{17,25},{10,2},{18,26},{11,3},{19,27},{12,4},{... | collective-permute-start | bytes 4718600 | tf_op jit(solution)/shard_map/ppermute | solution.py:801
  456.8 1.0 copy-start

commit v3 on v2

--- a/solution.py
+++ b/solution.py
@@ -17,9 +17,10 @@
 MESH = pl.DeviceIdType.MESH
 CHUNKS = 16
 PIECES = 4
+STAGGER = 3
 UNIT = 128
 EARLY = 4
-LATE = 6
+LATE = 7
 PAIR = 8
 TOGETHER = 4
 VMEM_LIMIT = 60 * 2**20
@@ -108,6 +109,7 @@
     wkv_stage_recv,
     help_send,
     help_recv,
+    turn,
 ):
     me = lax.axis_index("section")
     mine = lax.axis_index("tensor")
@@ -263,12 +265,15 @@
         )
 
     for side in range(2):
-        for p in range(PIECES):
-            pl.when(onward[side])(lambda: wkv_own_copy(side, p).start())
         pl.when(fed[side])(lambda: spread_copy(side).start())
     begin(wkv_copy, 0)
     begin(page_copy, 0)
-    ahead = min(kept, CHUNKS * 3 // 8)
+    second = lax.rem(mine, 2) == 1
+    pl.when(second)(lambda: pl.semaphore_wait(turn, 1))
+    for side in range(2):
+        for p in range(PIECES):
+            pl.when(onward[side])(lambda: wkv_own_copy(side, p).start())
+    ahead = CHUNKS * 3 // 8
     each_chunk(send_own, 0, ahead)
     for step in range(sections - 1, 0, -1):
         for side in range(2):
@@ -278,6 +283,13 @@
                 ).start()
             )
     each_chunk(send_own, ahead)
+
+    @pl.when(jnp.logical_not(second))
+    def _():
+        for side in range(2):
+            for p in range(STAGGER):
+                pl.when(onward[side])(lambda: wkv_own_copy(side, p).wait_send())
+        pl.semaphore_signal(turn, 1, device_id=(me, mine + 1), device_id_type=MESH)
 
     take = pltpu.make_async_copy(
         wq_ref.at[pl.ds(depth - late_rows, late_rows), :], held, local_sem.at[2]
@@ -384,7 +396,9 @@
     each_chunk(sent)
     for side in range(2):
         for p in range(PIECES):
-            pl.when(onward[side])(lambda: wkv_own_copy(side, p).wait_send())
+            pl.when(jnp.logical_and(onward[side], jnp.logical_or(second, p >= STAGGER)))(
+                lambda: wkv_own_copy(side, p).wait_send()
+            )
             for step in range(1, sections):
                 pl.when(jnp.logical_and(real(side, step), onward[side]))(
                     lambda: wkv_relay_copy(owner_of(side, step), side, p).wait_send()
@@ -469,6 +483,7 @@
             dma((sections, PIECES)),
             dma((3,)),
             dma((3,)),
+            pltpu.SemaphoreType.REGULAR,
         ],
         compiler_params=pltpu.CompilerParams(
             has_side_effects=True, vmem_limit_bytes=VMEM_LIMIT

time: 493 us -> 489 us (level); the launches traced: 493 us -> 480 us
  Pallas kernels: 475 us -> 462 us
    pallas_call x1, Pallas kernels: 432 us -> 419 us  [exchange(): pl.pallas_call(functools.partial(exchange_kernel, sections, tensors, loca...]
where the time goes in v3:
time: 489 us; the launch traced here: 480 us
  Pallas kernels  462 us (94%)
  other arithmetic  8.04 us (2%)
  local copies, waits for them, and re-layouts  5.72 us (1%)
    pallas_call x1, Pallas kernels, exchange(): pl.pallas_call(functools.partial(exchange_kernel, sections, tensors, loca...  419 us
    pallas_call x1, Pallas kernels, gather(): pl.pallas_call(functools.partial(gather_kernel, sections, tiles, tiles -...  18.6 us
    pallas_call x1, Pallas kernels, attend(): pl.pallas_call(functools.partial(attend_kernel, pages_of, together, page,...  11 us
    pallas_call x1, Pallas kernels, pick_pages(): pl.pallas_call(functools.partial(pick_kernel, count), out_shape=jax.Shape...  10 us
  transfers between devices with their start and end apart: 2, of which 0 were waited for; matrix products, arithmetic and copies ran while one was open for 3% of the time, Pallas kernels for 96%

profile of v3, /device:TPU:0, one launch (start us, length us, event | category | flops | bytes accessed | tf_op | source)
XLA Modules:
  0.0 479.6 jit_solution(7032397269301087952)
XLA Ops:
  0.7 2.2 take_rows.1
  2.9 1.3 collective-permute-start
  4.3 0.1 copy.28
  4.4 2.3 select_reduce_fusion.1
  6.6 0.2 fusion.4
  6.8 0.1 copy.31
  6.9 0.1 copy.30
  7.0 0.8 fusion.6.normed_ref
  7.9 2.2 select_reduce_fusion
  10.1 0.7 reshape.172.spots_ref
  10.8 10.0 %pick_pages.1.pages_ref = bf16[4,2,128,16,256]{4,3,2,1,0:T(8,128)(2,1)} custom-call(s32[512]{0:T(512)} %reshape.172.spots_ref, bf16[2,512,16,256]{3,2,1,0:T(8,128)(2,1)} %kv_ref.1), custom_call_target="tpu_custom_call" | custom-call | tf_op jit(solution)/shard_map/pick_pages/pallas_call | solution.py:60
  20.8 419.3 %exchange.1 = (f32[16,1024]{1,0:T(8,128)}, bf16[8,128,16,256]{3,2,1,0:T(8,128)(2,1)}, bf16[8192,256]{1,0:T(8,128)(2,1)}, bf16[8192,1024]{1,0:T(8,128)(2,1)}, bf1...) custom-call(bf16[16,8192]{1,0:T(8,128)(2,1)} %fusion.6.normed_ref, ...), custom_call_target="tpu_custom_call" | custom-call | flops 58720256 | bytes 419430400 | tf_op jit(solution)/shard_map/exchange/pallas_call | solution.py:451
  440.1 1.3 collective-permute-start.1
  441.4 0.7 reshape.170.block_ref
  442.1 0.1 constant_dynamic-slice_fusion
  442.2 0.1 copy.29
  442.2 0.7 reshape.171.spot_ref
  442.9 0.6 fusion.10
  443.6 0.1 multiply_cosine_fusion
  443.7 0.0 copy-start
  443.7 1.0 copy-done
  444.7 18.6 %gather_query.1 = (bf16[8192,1024]{1,0:T(8,128)(2,1)}, f32[16,1024]{1,0:T(8,128)}, bf16[8192,256]{1,0:T(8,128)(2,1)}, f32[16,256]{1,0:T(8,128)}) custom-call(s32[1]{0:T(128)} %bitcast.1.me_ref, bf16[16,8192]{1,0:T(8,128)(2,1)} %fusion.6.normed_ref, f32[16,1024]{1,0:T(8,128)} %get-tuple-element.16.part_ref, bf16[2048,1024]{1,0:T(8,128)(2,1)} %own_ref.1, ...), custom_call_target="tpu_custom_call" | custom-call | flops 268435456 | bytes 33554432 | tf_op jit(solution)/shard_map/gather_query/pallas_call | solution.py:583
  463.3 0.7 slice.19
  464.0 0.7 fusion.9
  464.7 0.9 copy.35
  465.5 0.1 mul.126
  465.6 0.3 subtract_convert_fusion.1
  465.9 0.7 pad_maximum_fusion.1.fresh_ref
  466.6 0.1 subtract_convert_fusion
  466.7 0.7 pad_maximum_fusion.query_ref
  467.4 11.0 %attend.1 = (bf16[16,1024,256]{2,1,0:T(8,128)(2,1)}, bf16[16,1024]{1,0:T(8,128)(2,1)}) custom-call(s32[1024]{0:T(1024)} %reshape.170.block_ref, s32[1024]{0:T(1024)} %reshape.171.spot_ref, s32[16]{0:T(128)} %get-tuple-element.43.length_ref, bf16[8,16,8,16,256]{4,3,2,1,0:T(8,128)(2,1)} %bitcast.11, bf16[16,1,256]{2,1,0:T(2,128)(2,1)} %pad_maximum_fusion.1.fresh_ref, ...), custom_call_target="tpu_custom_call" | custom-call | flops 67108864 | bytes 16777216 | tf_op jit(solution)/shard_map/attend/pallas_call | solution.py:749
  478.4 1.2 place_late.1
  (16 shorter events, 0.1 us)
Async XLA Ops:
  0.6 3.6 copy-start.2
  0.6 6.0 %copy-start.1 = (bf16[16,8192]{1,0:T(8,128)(2,1)S(1)}, bf16[16,8192]{1,0:T(8,128)(2,1)}, u32[]{:S(2)}) copy-start(bf16[16,8192]{1,0:T(8,128)(2,1)} %param.7) | copy-start | bytes 786436
  0.7 6.4 %copy-start.3 = (f32[8192]{0:T(1024)S(1)}, f32[8192]{0:T(1024)}, u32[]{:S(2)}) copy-start(f32[8192]{0:T(1024)} %param.8) | copy-start | bytes 98308
  2.9 440.8 %collective-permute-start = (bf16[512,1024]{1,0:T(8,128)(2,1)}, bf16[512,1024]{1,0:T(8,128)(2,1)S(1)}, u32[]{:S(2)}, u32[]{:S(2)}) collective-permute-start(bf16[512,1024]{1,0:T(8,128)(2,1)} %take_rows.1), channel_id=1, source_target_pairs={{8,0},{16,24},{9,1},{17,25},{10,2},{18,26},{11,3},{19,27},{12,4},{... | collective-permute-start | bytes 3145736 | tf_op jit(solution)/shard_map/ppermute | solution.py:812
  20.8 422.2 %copy-start.4 = (s32[64]{0:T(128)S(1)}, s32[64]{0:T(128)}, u32[]{:S(2)}) copy-start(s32[64]{0:T(128)} %param.13) | copy-start | bytes 772
  440.1 38.2 %collective-permute-start.1 = (bf16[896,1024]{1,0:T(8,128)(2,1)}, bf16[896,1024]{1,0:T(8,128)(2,1)S(1)}, u32[]{:S(2)}, u32[]{:S(2)}) collective-permute-start(bf16[896,1024]{1,0:T(8,128)(2,1)} %get-tuple-element.23), channel_id=1, source_target_pairs={{8,0},{16,24},{9,1},{17,25},{10,2},{18,26},{11,3},{19,27},{12,4},{... | collective-permute-start | bytes 5505032 | tf_op jit(solution)/shard_map/ppermute | solution.py:816
  443.7 1.0 copy-start

commit v4 on v3

--- a/solution.py
+++ b/solution.py
@@ -51,7 +51,7 @@
         out_ref[0, 0, i] = kv_ref[0, spots_ref[base + i]]
         return carry
 
-    lax.fori_loop(0, count, step, 0, unroll=8)
+    lax.fori_loop(0, count, step, 0, unroll=32)
 
 
 def pick_pages(kv_old, spots, sections):
@@ -273,7 +273,7 @@
     for side in range(2):
         for p in range(PIECES):
             pl.when(onward[side])(lambda: wkv_own_copy(side, p).start())
-    ahead = CHUNKS * 3 // 8
+    ahead = CHUNKS * 6 // 8
     each_chunk(send_own, 0, ahead)
     for step in range(sections - 1, 0, -1):
         for side in range(2):
@@ -667,15 +667,21 @@
     )(late, wq_new)
 
 
-def take_kernel(start, from_ref, out_ref, done):
-    copy = pltpu.make_async_copy(from_ref.at[pl.ds(start, out_ref.shape[0]), :], out_ref, done)
-    copy.start()
-    copy.wait()
-
-
-def take_rows(array, start, rows):
+def take_kernel(sections, start, from_ref, out_ref, done):
+    me = lax.axis_index("section")
+
+    @pl.when(jnp.logical_or(me == 1, me == sections - 2))
+    def _():
+        copy = pltpu.make_async_copy(
+            from_ref.at[pl.ds(start, out_ref.shape[0]), :], out_ref, done
+        )
+        copy.start()
+        copy.wait()
+
+
+def take_rows(array, start, rows, sections):
     return pl.pallas_call(
-        functools.partial(take_kernel, start),
+        functools.partial(take_kernel, sections, start),
         out_shape=jax.ShapeDtypeStruct((rows, array.shape[1]), array.dtype),
         in_specs=[pl.BlockSpec(memory_space=pl.ANY)],
         out_specs=pl.BlockSpec(memory_space=pltpu.VMEM),
@@ -697,7 +703,7 @@
             cache_ref[r, pl.ds(start, page), :] = in_ref[block_ref[at], r, spot_ref[at]]
         return carry
 
-    lax.fori_loop(0, pages_of, order, 0, unroll=8)
+    lax.fori_loop(0, pages_of, order, 0, unroll=16)
     for r in range(together):
         length = length_ref[step * together + r]
         start = pl.multiple_of(lax.div(length, page) * page, page)
@@ -807,7 +813,7 @@
     ends = sorted({(sections - 2, sections - 1), (1, 0)})
     tiles, early_tiles, late_tiles = split(depth)
     early = take_rows(
-        wq_old, (tiles - early_tiles - late_tiles) * UNIT, early_tiles * UNIT
+        wq_old, (tiles - early_tiles - late_tiles) * UNIT, early_tiles * UNIT, sections
     )
     early = lax.ppermute(early, "section", ends)
     part, arrived, wkv_far, far, _, _, late = exchange(

time: 489 us -> 487 us (level)
  no operation moved by 1% of the time
where the time goes in v4:
time: 487 us; the launch traced here: 478 us
  Pallas kernels  461 us (95%)
  other arithmetic  8.04 us (2%)
  local copies, waits for them, and re-layouts  5.72 us (1%)
    pallas_call x1, Pallas kernels, exchange(): pl.pallas_call(functools.partial(exchange_kernel, sections, tensors, loca...  419 us
    pallas_call x1, Pallas kernels, gather(): pl.pallas_call(functools.partial(gather_kernel, sections, tiles, tiles -...  18.6 us
    pallas_call x1, Pallas kernels, attend(): pl.pallas_call(functools.partial(attend_kernel, pages_of, together, page,...  10.8 us
    pallas_call x1, Pallas kernels, pick_pages(): pl.pallas_call(functools.partial(pick_kernel, count), out_shape=jax.Shape...  9.79 us
  transfers between devices with their start and end apart: 2, of which 0 were waited for; matrix products, arithmetic and copies ran while one was open for 3% of the time, Pallas kernels for 96%

profile of v4, /device:TPU:0, one launch (start us, length us, event | category | flops | bytes accessed | tf_op | source)
XLA Modules:
  0.0 477.9 jit_solution(15904054634656021526)
XLA Ops:
  0.7 1.0 take_rows.1
  1.7 1.3 collective-permute-start
  3.0 0.1 copy.28
  3.1 2.3 select_reduce_fusion.1
  5.4 0.2 fusion.4
  5.6 0.1 copy.31
  5.7 0.1 copy.30
  5.8 0.8 fusion.6.normed_ref
  6.6 2.2 select_reduce_fusion
  8.8 0.7 reshape.172.spots_ref
  9.5 9.8 %pick_pages.1.pages_ref = bf16[4,2,128,16,256]{4,3,2,1,0:T(8,128)(2,1)} custom-call(s32[512]{0:T(512)} %reshape.172.spots_ref, bf16[2,512,16,256]{3,2,1,0:T(8,128)(2,1)} %kv_ref.1), custom_call_target="tpu_custom_call" | custom-call | tf_op jit(solution)/shard_map/pick_pages/pallas_call | solution.py:60
  19.3 419.3 %exchange.1 = (f32[16,1024]{1,0:T(8,128)}, bf16[8,128,16,256]{3,2,1,0:T(8,128)(2,1)}, bf16[8192,256]{1,0:T(8,128)(2,1)}, bf16[8192,1024]{1,0:T(8,128)(2,1)}, bf1...) custom-call(bf16[16,8192]{1,0:T(8,128)(2,1)} %fusion.6.normed_ref, ...), custom_call_target="tpu_custom_call" | custom-call | flops 58720256 | bytes 419430400 | tf_op jit(solution)/shard_map/exchange/pallas_call | solution.py:451
  438.6 1.3 collective-permute-start.1
  440.0 0.7 reshape.170.block_ref
  440.6 0.1 constant_dynamic-slice_fusion
  440.7 0.1 copy.29
  440.8 0.7 reshape.171.spot_ref
  441.5 0.6 fusion.10
  442.1 0.1 multiply_cosine_fusion
  442.2 0.0 copy-start
  442.2 1.0 copy-done
  443.2 18.6 %gather_query.1 = (bf16[8192,1024]{1,0:T(8,128)(2,1)}, f32[16,1024]{1,0:T(8,128)}, bf16[8192,256]{1,0:T(8,128)(2,1)}, f32[16,256]{1,0:T(8,128)}) custom-call(s32[1]{0:T(128)} %bitcast.1.me_ref, bf16[16,8192]{1,0:T(8,128)(2,1)} %fusion.6.normed_ref, f32[16,1024]{1,0:T(8,128)} %get-tuple-element.16.part_ref, bf16[2048,1024]{1,0:T(8,128)(2,1)} %own_ref.1, ...), custom_call_target="tpu_custom_call" | custom-call | flops 268435456 | bytes 33554432 | tf_op jit(solution)/shard_map/gather_query/pallas_call | solution.py:583
  461.8 0.7 slice.19
  462.5 0.7 fusion.9
  463.2 0.9 copy.35
  464.1 0.1 mul.126
  464.2 0.3 subtract_convert_fusion.1
  464.4 0.7 pad_maximum_fusion.1.fresh_ref
  465.1 0.1 subtract_convert_fusion
  465.2 0.7 pad_maximum_fusion.query_ref
  465.9 10.8 %attend.1 = (bf16[16,1024,256]{2,1,0:T(8,128)(2,1)}, bf16[16,1024]{1,0:T(8,128)(2,1)}) custom-call(s32[1024]{0:T(1024)} %reshape.170.block_ref, s32[1024]{0:T(1024)} %reshape.171.spot_ref, s32[16]{0:T(128)} %get-tuple-element.43.length_ref, bf16[8,16,8,16,256]{4,3,2,1,0:T(8,128)(2,1)} %bitcast.11, bf16[16,1,256]{2,1,0:T(2,128)(2,1)} %pad_maximum_fusion.1.fresh_ref, ...), custom_call_target="tpu_custom_call" | custom-call | flops 67108864 | bytes 16777216 | tf_op jit(solution)/shard_map/attend/pallas_call | solution.py:755
  476.7 1.2 place_late.1
  (16 shorter events, 0.1 us)
Async XLA Ops:
  0.6 2.3 copy-start.2
  0.6 4.7 copy-start.1
  0.7 5.1 %copy-start.3 = (f32[8192]{0:T(1024)S(1)}, f32[8192]{0:T(1024)}, u32[]{:S(2)}) copy-start(f32[8192]{0:T(1024)} %param.8) | copy-start | bytes 98308
  1.7 440.6 %collective-permute-start = (bf16[512,1024]{1,0:T(8,128)(2,1)}, bf16[512,1024]{1,0:T(8,128)(2,1)S(1)}, u32[]{:S(2)}, u32[]{:S(2)}) collective-permute-start(bf16[512,1024]{1,0:T(8,128)(2,1)} %take_rows.1), channel_id=1, source_target_pairs={{8,0},{16,24},{9,1},{17,25},{10,2},{18,26},{11,3},{19,27},{12,4},{... | collective-permute-start | bytes 3145736 | tf_op jit(solution)/shard_map/ppermute | solution.py:818
  19.3 422.2 %copy-start.4 = (s32[64]{0:T(128)S(1)}, s32[64]{0:T(128)}, u32[]{:S(2)}) copy-start(s32[64]{0:T(128)} %param.13) | copy-start | bytes 772
  438.6 38.0 %collective-permute-start.1 = (bf16[896,1024]{1,0:T(8,128)(2,1)}, bf16[896,1024]{1,0:T(8,128)(2,1)S(1)}, u32[]{:S(2)}, u32[]{:S(2)}) collective-permute-start(bf16[896,1024]{1,0:T(8,128)(2,1)} %get-tuple-element.23), channel_id=1, source_target_pairs={{8,0},{16,24},{9,1},{17,25},{10,2},{18,26},{11,3},{19,27},{12,4},{... | collective-permute-start | bytes 5505032 | tf_op jit(solution)/shard_map/ppermute | solution.py:822
  442.2 1.0 copy-start
